TPU v7x, 32 devices: a whole 2x2x4 slice. The times are simulated.
32 devices in a mesh: dp: 4 (over z), tp: 8 (over y, x, core).
Axes of the slice: x: 2, y: 2, z: 4, core: 2. Of those that a mesh axis runs over, the one named last changes fastest.
Arguments:
- token_ids: int32 [32768], P('dp'), parts along dimension 0
- positions: int32 [32768], P('dp'), parts along dimension 0
- embed_table: bfloat16 [257216, 2048], P('tp')
- norm_scale: float32 [2048], replicated
- w_query: bfloat16 [2048, 2048], P(None, 'tp')
- w_key: bfloat16 [2048, 256], replicated
- w_value: bfloat16 [2048, 256], replicated
Outputs:
- output 1: bfloat16 [32768, 2048], P(('dp', 'tp')), parts along dimension 0
- output 2: bfloat16 [32768, 8, 256], P('dp', 'tp'), parts along dimension 0
- output 3: bfloat16 [32768, 8, 256], P('dp', 'tp'), parts along dimension 0
- output 4: bfloat16 [32768, 8, 256], P('dp', 'tp'), parts along dimension 0
There are 4 independent parts. A program takes and returns all parts, laid end to end along the dimension named above; an argument that names none is the same for every part.
All inputs are finite; a program needn't handle non-finite values.
Results may differ from a plain program's by a relative error of at most 0.0120334.
Values are sent between devices in bfloat16 or wider.
A program may use at most 1 GiB of HBM per device.

v0:
```python
import math
import jax
import jax.numpy as jnp
from jax import lax
from jax.sharding import PartitionSpec as P

HEAD_DIM = 256
EPSILON = 1e-6
ROPE_BASE = 10000.0


def rope_tables(positions):
    inv_freq = ROPE_BASE ** (-jnp.arange(0, HEAD_DIM, 2, dtype=jnp.float32) / HEAD_DIM)
    angles = positions.astype(jnp.float32)[:, None] * inv_freq[None, :]
    return jnp.cos(angles)[:, None, :], jnp.sin(angles)[:, None, :]


def rotate(head_vals, cosines, sines):
    half_dim = head_vals.shape[-1] // 2
    front_half = head_vals[..., :half_dim]
    back_half = head_vals[..., half_dim:]
    return jnp.concatenate([front_half * cosines - back_half * sines, back_half * cosines + front_half * sines], axis=-1)


def rms_norm(resid_rows, norm_scale):
    widened = resid_rows.astype(jnp.float32)
    inv_rms = lax.rsqrt(jnp.mean(widened * widened, axis=-1, keepdims=True) + EPSILON)
    return (widened * inv_rms * (1.0 + norm_scale)).astype(jnp.bfloat16)


def project(normed, weight, cosines, sines, factor):
    linear = jnp.dot(normed, weight, preferred_element_type=jnp.float32).astype(jnp.bfloat16)
    head_view = linear.reshape(linear.shape[0], -1, HEAD_DIM).astype(jnp.float32)
    return (rotate(head_view, cosines, sines) * factor).astype(jnp.bfloat16)


def solution(mesh):
    group_size = mesh.shape["tp"]

    def local_step(token_ids, positions, table_rows, norm_scale, w_query, w_key, w_value):
        dev_index = lax.axis_index("tp")
        vocab_rows, model_width = table_rows.shape
        normalizer = jnp.asarray(math.sqrt(model_width), dtype=jnp.bfloat16)
        local_ids = token_ids - dev_index * vocab_rows
        inside = (local_ids >= 0) & (local_ids < vocab_rows)
        picked = jnp.take(table_rows, local_ids, axis=0, mode="clip") * normalizer
        partial = jnp.where(inside[:, None], picked, jnp.zeros((), jnp.bfloat16))
        residual = lax.psum_scatter(partial, "tp", scatter_dimension=0, tiled=True)
        normed = lax.all_gather(rms_norm(residual, norm_scale), "tp", axis=0, tiled=True)
        cosines, sines = rope_tables(positions)
        queries = project(normed, w_query, cosines, sines, HEAD_DIM ** -0.5)
        kv_heads = w_key.shape[1] // HEAD_DIM
        slot_count = max(kv_heads, group_size)
        slots_here = slot_count // group_size
        first_head = (dev_index * slots_here) // (slot_count // kv_heads)
        key_cols = lax.dynamic_slice_in_dim(w_key, first_head * HEAD_DIM, slots_here * HEAD_DIM, axis=1)
        value_cols = lax.dynamic_slice_in_dim(w_value, first_head * HEAD_DIM, slots_here * HEAD_DIM, axis=1)
        key_heads = project(normed, key_cols, cosines, sines, 1.0)
        value_lin = jnp.dot(normed, value_cols, preferred_element_type=jnp.float32).astype(jnp.bfloat16)
        value_heads = value_lin.reshape(value_lin.shape[0], slots_here, HEAD_DIM)
        return residual, queries, key_heads, value_heads

    head_spec = P("dp", "tp", None)
    return jax.shard_map(local_step, mesh=mesh, in_specs=(P("dp"), P("dp"), P("tp", None), P(), P(None, "tp"), P(), P()), out_specs=(P(("dp", "tp"), None), head_spec, head_spec, head_spec), check_vma=False)
```

profile of v0, /device:TPU:15, one launch (start us, length us, event | category | flops | bytes accessed | tf_op | source)
XLA Modules:
  0.0 942.4 jit_solution(1854523864326944309)
XLA Ops:
  7.2 0.0 copy-start
  7.2 0.0 reduce-scatter.2.cloned.1.call-start
  7.2 0.8 compare_and_fusion
  8.1 0.8 subtract_clamp_fusion
  8.9 438.8 %gather_fusion = bf16[8192,2048]{1,0:T(8,128)(2,1)} fusion(bf16[32152,2048]{1,0:T(8,128)(2,1)} %param.9, s32[8192]{0:T(1024)S(1)} %subtract_clamp_fusion), kind=kCustom, calls=%fused_computation | custom fusion | bytes 67141632 | tf_op jit(solution)/shard_map/jit(_take)/gather | solution.py:46
  447.7 22.9 %multiply_select_fusion = bf16[8192,2048]{1,0:T(8,128)(2,1)} fusion(bf16[8192,2048]{1,0:T(8,128)(2,1)} %gather_fusion, pred[8192]{0:T(1024)(128)(4,1)S(1)} %compare_and_fusion), kind=kLoop, calls=%fused_computation.1 | loop fusion | flops 33554432 | bytes 67117056 | tf_op jit(solution)/shard_map/jit(_where)/select_n | solution.py:47
  470.5 0.0 copy-start.3
  470.5 0.0 reduce-scatter.2.cloned.1.call-update
  470.5 0.0 all-gather.2.cloned.1.call-start
  470.6 0.6 copy-done.3
  471.2 204.1 %reduce-scatter.2.cloned.1.call-done = bf16[1024,2048]{1,0:T(8,128)(2,1)} async-done(((bf16[8192,2048]{1,0:T(8,128)(2,1)}), bf16[1024,2048]{1,0:T(8,128)(2,1)}) %reduce-scatter.2.cloned.1.call-update) | async-done | bytes 4194320 | tf_op jit(solution)/shard_map/reduce_scatter | solution.py:48
  675.4 0.0 copy-start.1
  675.4 3.2 fusion.5
  678.6 0.2 copy-done.1
  678.8 3.0 fusion.7
  681.9 0.0 copy-start.2
  681.9 0.0 all-gather.2.cloned.1.call-update
  681.9 0.7 copy-done.2
  682.6 0.0 copy-start.4
  682.6 160.8 %all-gather.2.cloned.1.call-done = bf16[8192,2048]{1,0:T(8,128)(2,1)} async-done(((bf16[1024,2048]{1,0:T(8,128)(2,1)}), bf16[8192,2048]{1,0:T(8,128)(2,1)}) %all-gather.2.cloned.1.call-update) | async-done | bytes 33554448 | tf_op jit(solution)/shard_map/all_gather | solution.py:49
  843.5 0.0 copy-done
  843.5 17.5 %fusion.3 = f32[8192,1,256]{0,2,1:T(8,128)} fusion(bf16[8192,2048]{1,0:T(8,128)(2,1)} %all-gather.2.cloned.1.call-done, bf16[2048,256]{1,0:T(8,128)(2,1)S(1)} %copy-done), kind=kOutput, calls=%fused_computation.10 | convolution fusion | flops 8594128896 | bytes 42991616 | tf_op jit(solution)/shard_map/dot_general | solution.py:32
  861.0 0.0 copy-done.4
  861.0 17.5 %fusion.1 = f32[8192,1,256]{0,2,1:T(8,128)} fusion(bf16[8192,2048]{1,0:T(8,128)(2,1)} %all-gather.2.cloned.1.call-done, bf16[2048,256]{1,0:T(8,128)(2,1)S(1)} %copy-done.4), kind=kOutput, calls=%fused_computation.8 | convolution fusion | flops 8594128896 | bytes 42991616 | tf_op jit(solution)/shard_map/dot_general | solution.py:32
  878.5 20.2 %fusion.20 = (bf16[8192,1,128]{0,2,1:T(8,128)(2,1)S(1)}, bf16[8192,1,128]{0,2,1:T(8,128)(2,1)S(1)}, f32[8192,1,128]{0,2,1:T(8,128)}, f32[8192,1,128]{0,2,1:T(8,128)}) fusion(f32[8192,1,256]{0,2,1:T(8,128)} %fusion.3, f32[128]{0:T(128)S(1)} %multiply_power_fusion, f32[8192]{0:T(1024)S(1)} %convert_element_type.55, f32[8192,1,256]{0,2,1:T(8,128)} %fusion.1), kind=kLoop, calls=%fused_computation.30 | loop fusion | flops 15728640 | bytes 29393408 | tf_op jit(solution)/shard_map/convert.2
  898.7 2.5 pad_maximum_fusion
  901.2 6.4 copy.12
  907.5 5.1 fusion.8
  912.7 0.0 copy-start.5
  912.7 6.4 copy.11
  919.1 0.0 copy-done.5
  919.1 16.4 %fusion.4 = bf16[8192,1,256]{2,0,1:T(8,128)(2,1)} fusion(bf16[8192,2048]{1,0:T(8,128)(2,1)} %all-gather.2.cloned.1.call-done, bf16[2048,256]{1,0:T(8,128)(2,1)S(1)} %copy-done.5), kind=kOutput, calls=%fused_computation.11 | convolution fusion | flops 8592031744 | bytes 38797312 | tf_op jit(solution)/shard_map/dot_general | solution.py:59
  (4 shorter events, 0.0 us)
Async XLA Ops:
  7.2 836.3 %copy-start = (bf16[2048,256]{1,0:T(8,128)(2,1)S(1)}, bf16[2048,256]{1,0:T(8,128)(2,1)}, u32[]{:S(2)}) copy-start(bf16[2048,256]{1,0:T(8,128)(2,1)} %param.12) | copy-start | bytes 3145732
  7.2 668.2 %reduce-scatter.2.cloned.1.call-start = ((), (), s32[]{:S(2)}) async-start(), calls=%async_computation.1 | async-start | bytes 37748736 | tf_op jit(solution)/shard_map/reduce_scatter | solution.py:48
  470.5 0.7 copy-start.3
  470.5 372.9 %all-gather.2.cloned.1.call-start = ((), (), s32[]{:S(2)}) async-start(), calls=%async_computation.2 | async-start | bytes 37748736 | tf_op jit(solution)/shard_map/all_gather | solution.py:49
  675.4 3.4 copy-start.1
  681.9 0.8 copy-start.2
  682.6 178.4 %copy-start.4 = (bf16[2048,256]{1,0:T(8,128)(2,1)S(1)}, bf16[2048,256]{1,0:T(8,128)(2,1)}, u32[]{:S(2)}) copy-start(bf16[2048,256]{1,0:T(8,128)(2,1)} %param.11) | copy-start | bytes 3145732
  912.7 6.5 copy-start.5
Sparse Core Ops, SparseCore 0:
  470.7 204.6 reduce-scatter.1
  682.0 161.4 all-gather.1
where the time goes:
time: 952 us; the launch traced here: 942 us
  local copies, waits for them, and re-layouts  453 us (48%)
  waiting for transfers between devices  365 us (38%)
  other arithmetic  58.6 us (6%)
  matrix products  51.4 us (5%)
  between operations  14.1 us (1%)
    gather x1, local copies, waits for them, and re-layouts, local_step(): picked = jnp.take(table_rows, local_ids, axis=0, mode='clip') * normalizer  439 us
    reduce_scatter x1, waiting for transfers between devices, local_step(): residual = lax.psum_scatter(partial, 'tp', scatter_dimension=0, tiled=True)  204 us
    all_gather x1, waiting for transfers between devices, local_step(): lax.all_gather(rms_norm(residual, norm_scale), 'tp', axis=0, tiled=True)  161 us
    dot_general x2, matrix products, project(): jnp.dot(normed, weight, preferred_element_type=jnp.float32)  35 us
    select_n x1, other arithmetic, local_step(): partial = jnp.where(inside[:, None], picked, jnp.zeros((), jnp.bfloat16))  22.9 us
    another operation x1, other arithmetic  20.2 us
  transfers between devices with their start and end apart: 2, of which 2 were waited for; matrix products, arithmetic and copies ran while one was open for 0% of the time, Pallas kernels for 0%

commit v1 on v0

v1 whole, which is shorter than its diff:
```python
import functools
import math

import jax
import numpy as np
import jax.numpy as jnp
from jax import lax
from jax.experimental import pallas as pl
from jax.experimental.pallas import tpu as pltpu
from jax.sharding import PartitionSpec as P

HEAD_DIM = 256
EPSILON = 1e-6
ROPE_BASE = 10000.0
MESH = pl.DeviceIdType.MESH
BF16, F32, I32 = jnp.bfloat16, jnp.float32, jnp.int32

HOT = 1024
LIST_CAP = (2816, 640, 352, 352, 192, 192, 192, 192)
CHUNK = (64, 64, 32, 32, 32, 32, 32, 32)
SEG_ROWS = tuple(c + (HOT if d == 0 else 0) for d, c in enumerate(LIST_CAP))
SEG_BASE = tuple(sum(SEG_ROWS[:d]) for d in range(8))
TOTAL = sum(SEG_ROWS)
ROWS = -(-TOTAL // 256) * 256
SEG_CHUNKS = tuple(r // c for r, c in zip(SEG_ROWS, CHUNK))
CHUNK_ID = tuple(sum(SEG_CHUNKS[:d]) for d in range(8))
ALL_CHUNKS = sum(SEG_CHUNKS)
SPLIT = 35
LIST_LEN = 3072
RING = ((0, 1, 3, 2), (0, 2, 3, 1))


def rope_tables(positions):
    inv_freq = ROPE_BASE ** (-jnp.arange(0, HEAD_DIM, 2, dtype=F32) / HEAD_DIM)
    angles = positions.astype(F32)[:, None] * inv_freq[None, :]
    return jnp.cos(angles), jnp.sin(angles)


def rotate(head_vals, cosines, sines):
    half_dim = head_vals.shape[-1] // 2
    front_half = head_vals[..., :half_dim]
    back_half = head_vals[..., half_dim:]
    return jnp.concatenate([front_half * cosines - back_half * sines, back_half * cosines + front_half * sines], axis=-1)


def rms_norm(resid_rows, norm_scale):
    widened = resid_rows.astype(F32)
    inv_rms = lax.rsqrt(jnp.mean(widened * widened, axis=-1, keepdims=True) + EPSILON)
    return (widened * inv_rms * (1.0 + norm_scale)).astype(BF16)


def dense_step(token_ids, positions, table_rows, norm_scale, w_query, w_key, w_value):
    vocab_rows, model_width = table_rows.shape
    normalizer = jnp.asarray(math.sqrt(model_width), dtype=BF16)
    local_ids = token_ids - lax.axis_index("tp") * vocab_rows
    inside = (local_ids >= 0) & (local_ids < vocab_rows)
    picked = jnp.take(table_rows, local_ids, axis=0, mode="clip") * normalizer
    partial = jnp.where(inside[:, None], picked, jnp.zeros((), BF16))
    residual = lax.psum_scatter(partial, "tp", scatter_dimension=0, tiled=True)
    normed = lax.all_gather(rms_norm(residual, norm_scale), "tp", axis=0, tiled=True)
    cosines, sines = rope_tables(positions)

    def project(weight, factor):
        linear = jnp.dot(normed, weight, preferred_element_type=F32).astype(BF16).astype(F32)
        return (rotate(linear, cosines, sines) * factor).astype(BF16)

    value_heads = jnp.dot(normed, w_value, preferred_element_type=F32).astype(BF16)
    return residual, project(w_query, HEAD_DIM ** -0.5), project(w_key, 1.0), value_heads


def plan(token_ids, vocab_rows, me):
    tokens = token_ids.shape[0]
    lanes = 128
    ids = token_ids.reshape(tokens // lanes, lanes)
    owner = ids // vocab_rows
    hot = ids < HOT
    mine = jnp.where(hot, 8, owner)
    onehot = mine[None] == jnp.arange(8, dtype=I32)[:, None, None]
    marks = onehot.astype(BF16)
    upper = (jnp.arange(lanes)[:, None] < jnp.arange(lanes)[None, :]).astype(BF16)
    within = jnp.einsum("orl,lm->orm", marks, upper, preferred_element_type=F32)
    per_row = jnp.sum(onehot.astype(F32), axis=-1)
    rows = tokens // lanes
    lower = (jnp.arange(rows)[None, :] < jnp.arange(rows)[:, None]).astype(F32)
    before = jnp.sum(lower[None] * per_row[:, None, :], axis=-1)
    counts = jnp.sum(per_row, axis=-1).astype(I32)
    place = (within + before[:, :, None]).astype(I32)
    bases = jnp.asarray([SEG_BASE[d] + (HOT if d == 0 else 0) for d in range(8)], I32)
    index = jnp.sum(jnp.where(onehot, place + bases[:, None, None], 0), axis=0)
    index = jnp.where(hot, ids, index).reshape(tokens)
    caps = jnp.asarray(LIST_CAP, I32)
    fits = jnp.all(counts <= caps)
    index = jnp.minimum(index, ROWS - 1)

    own = mine == me
    own_place = jnp.sum(jnp.where(onehot, place, 0), axis=0).reshape(tokens)
    own = own.reshape(tokens)
    local = jnp.where(own, token_ids - me * vocab_rows, 0)
    tall = LIST_LEN // 64
    high = (own[:, None] & (own_place[:, None] // 64 == jnp.arange(tall)[None, :])).astype(BF16)
    low = (own_place[:, None] % 64 == jnp.arange(64)[None, :]).astype(F32)
    values = jnp.concatenate([low * (local // 256).astype(F32)[:, None], low * (local % 256).astype(F32)[:, None]], axis=1)
    table = lax.dot_general(high, values.astype(BF16), (((0,), (0,)), ((), ())), preferred_element_type=F32)
    own_list = (table[:, :64] * 256 + table[:, 64:]).astype(I32).reshape(LIST_LEN)
    count = jnp.minimum(jnp.sum(own.astype(I32)), caps[me])
    return index, own_list, count, fits


STEP = 128


def gather_kernel(scale, params, rows_list, lanes_list, source, out, groups, picked, in_sems, out_sems):
    hot_steps, steps, base = params[0], params[1], params[2]
    end = hot_steps + steps

    def issue(step, slot):
        @pl.when(step < hot_steps)
        def _():
            pltpu.make_async_copy(source.at[pl.ds(pl.multiple_of(step * STEP, STEP), STEP)], groups.at[slot, pl.ds(0, STEP)], in_sems.at[slot]).start()

        @pl.when(step >= hot_steps)
        def _():
            def one(t, _):
                group = lax.div(rows_list[(step - hot_steps) * STEP + t], 8)
                pltpu.make_async_copy(source.at[pl.ds(pl.multiple_of(group * 8, 8), 8)], groups.at[slot, pl.ds(pl.multiple_of(t * 8, 8), 8)], in_sems.at[slot]).start()
                return 0

            lax.fori_loop(0, STEP, one, 0, unroll=8)

    def drain(slot):
        pltpu.make_async_copy(picked.at[slot], out.at[pl.ds(0, STEP)], out_sems.at[slot]).wait()

    @pl.when(end > 0)
    def _():
        issue(0, 0)

    def body(step, _):
        slot = lax.rem(step, 2)

        @pl.when(step + 1 < end)
        def _():
            issue(step + 1, 1 - slot)

        @pl.when(step >= 2)
        def _():
            drain(slot)

        @pl.when(step < hot_steps)
        def _():
            pltpu.make_async_copy(source.at[pl.ds(0, STEP)], groups.at[slot, pl.ds(0, STEP)], in_sems.at[slot]).wait()
            picked[slot] = groups[slot, :STEP, :]

        @pl.when(step >= hot_steps)
        def _():
            pltpu.make_async_copy(source.at[pl.ds(0, STEP * 8)], groups.at[slot], in_sems.at[slot]).wait()
            within = lax.rem(lanes_list[pl.ds(step - hot_steps, 1), :], 8)
            target = lax.broadcasted_iota(I32, (1, STEP), 1) * 8 + within
            target = jnp.broadcast_to(target, (STEP, STEP)).T
            lane = lax.broadcasted_iota(I32, (STEP, STEP), 1)
            select = jnp.concatenate([(lane + STEP * j == target).astype(F32).astype(BF16) for j in range(8)], axis=1)
            for c in range(0, 2048, 256):
                rows = jnp.dot(select, groups[slot, :, c:c + 256], preferred_element_type=F32)
                picked[slot, :, c:c + 256] = (rows if scale is None else rows * scale).astype(BF16)

        pltpu.make_async_copy(picked.at[slot], out.at[pl.ds(pl.multiple_of(base + step * STEP, 8), STEP)], out_sems.at[slot]).start()
        return 0

    lax.fori_loop(0, end, body, 0)

    @pl.when(end >= 2)
    def _():
        drain(lax.rem(end, 2))

    @pl.when(end >= 1)
    def _():
        drain(lax.rem(end + 1, 2))


def gather_rows(params, rows_list, source, out_rows, scale, name):
    return pl.pallas_call(
        functools.partial(gather_kernel, scale),
        out_shape=jax.ShapeDtypeStruct((out_rows, source.shape[1]), BF16),
        in_specs=[
            pl.BlockSpec(memory_space=pltpu.SMEM),
            pl.BlockSpec(memory_space=pltpu.SMEM),
            pl.BlockSpec(memory_space=pltpu.VMEM),
            pl.BlockSpec(memory_space=pl.ANY),
        ],
        out_specs=pl.BlockSpec(memory_space=pl.ANY),
        scratch_shapes=[
            pltpu.VMEM((2, STEP * 8, 2048), BF16),
            pltpu.VMEM((2, STEP, 2048), BF16),
            pltpu.SemaphoreType.DMA((2,)),
            pltpu.SemaphoreType.DMA((2,)),
        ],
        name=name,
    )(params, rows_list, rows_list.reshape(-1, STEP), source)


def ring_device(core, place):
    return 2 * RING[core][place % 4] + core


def ring_parts(core, place):
    if place % 4:
        device = ring_device(core, place)
        return [(device, 0, SEG_CHUNKS[device])]
    if core == 0:
        return [(0, 0, SPLIT)]
    return [(1, 0, SEG_CHUNKS[1]), (0, SPLIT, SEG_CHUNKS[0] - SPLIT)]


def broadcast_kernel(_, rows, ring_sems, pair_sems, recv_sems):
    me = lax.axis_index("tp")
    core, chip = me % 2, me // 2
    x, y = chip % 2, chip // 2
    along_x = 2 * (2 * y + 1 - x) + core
    along_y = 2 * (2 * (1 - y) + x) + core
    other = 2 * chip + 1 - core
    barrier = pltpu.get_barrier_semaphore()
    for peer in (along_x, along_y, other):
        pl.semaphore_signal(barrier, inc=1, device_id={"tp": peer}, device_id_type=MESH)
    pl.semaphore_wait(barrier, 3)

    def chunk(device, i):
        size = CHUNK[device]
        return rows.at[pl.ds(pl.multiple_of(SEG_BASE[device] + i * size, 8), size)], CHUNK_ID[device] + i

    def copy(device, i, sems, target):
        ref, number = chunk(device, i)
        return pltpu.make_async_remote_copy(
            src_ref=ref, dst_ref=ref, send_sem=sems.at[number], recv_sem=recv_sems.at[number],
            device_id={"tp": target}, device_id_type=MESH)

    def each(parts, fn):
        for device, first, number in parts:
            def body(i, _, device=device):
                fn(device, i)
                return 0

            lax.fori_loop(first, first + number, body, 0)

    def role(core, place):
        here = ring_device(core, place)
        after, pair = ring_device(core, place + 1), here ^ 1

        def to_ring(device, i):
            copy(device, i, ring_sems, after).start()

        def to_pair(device, i):
            copy(device, i, pair_sems, pair).start()

        def arrived(device, i):
            copy(device, i, ring_sems, after).wait_recv()

        def to_both(device, i):
            to_ring(device, i)
            to_pair(device, i)

        def arrive_to_both(device, i):
            arrived(device, i)
            to_both(device, i)

        def arrive_to_ring(device, i):
            arrived(device, i)
            to_ring(device, i)

        def arrive_to_pair(device, i):
            arrived(device, i)
            to_pair(device, i)

        own = [(here, 0, SEG_CHUNKS[here])]
        head = ring_parts(core, place)
        late = []
        if here == 0:
            late = ring_parts(1, 0)[1:]
            both = min(late[0][2], SPLIT)

            def interleave(i, _):
                to_pair(0, SPLIT + i)
                to_both(0, i)
                return 0

            lax.fori_loop(0, both, interleave, 0)
            each([(0, both, SPLIT - both)], to_both)
            each([(0, SPLIT + both, late[0][2] - both)], to_pair)
            sent_ring, sent_pair = list(head), list(own)
        elif here == 1:
            each(own, to_both)
            each(head[1:], arrive_to_ring)
            sent_ring, sent_pair = list(head), list(own)
        else:
            each(own, to_both)
            sent_ring, sent_pair = list(own), list(own)
        for back in (1, 2):
            parts = ring_parts(core, place - back)
            each(parts, arrive_to_both)
            sent_ring += parts
            sent_pair += parts
        parts = ring_parts(core, place - 3)
        each(parts, arrive_to_pair)
        sent_pair += parts
        pair_place = RING[1 - core].index(here // 2)
        if here == 1:
            from_pair = [(0, 0, SPLIT)]
        elif here == 0:
            from_pair = [(1, 0, SEG_CHUNKS[1])]
        else:
            from_pair = ring_parts(1 - core, pair_place)
        for back in (1, 2, 3):
            from_pair = from_pair + ring_parts(1 - core, pair_place - back)
        each(from_pair, arrived)
        each(sent_ring, lambda device, i: copy(device, i, ring_sems, after).wait_send())
        each(sent_pair, lambda device, i: copy(device, i, pair_sems, pair).wait_send())

    for core_here in range(2):
        for place_here in range(4):
            pl.when(me == ring_device(core_here, place_here))(functools.partial(role, core_here, place_here))


def broadcast_rows(rows):
    return pl.pallas_call(
        broadcast_kernel,
        out_shape=jax.ShapeDtypeStruct(rows.shape, rows.dtype),
        in_specs=[pl.BlockSpec(memory_space=pl.ANY)],
        out_specs=pl.BlockSpec(memory_space=pl.ANY),
        scratch_shapes=[
            pltpu.SemaphoreType.DMA((ALL_CHUNKS,)),
            pltpu.SemaphoreType.DMA((ALL_CHUNKS,)),
            pltpu.SemaphoreType.DMA((ALL_CHUNKS,)),
        ],
        input_output_aliases={0: 0},
        compiler_params=pltpu.CompilerParams(collective_id=0, has_side_effects=True),
        name="broadcast_rows",
    )(rows)


ROW_BLOCK = 256
TOKEN_BLOCK = 256
PITCH = ROWS + 8
OUT_PITCH = TOKEN_BLOCK + 8
ROW_STEPS = ROWS // ROW_BLOCK


def project_kernel(scale, index, rows, norm_scale, w_query, w_key, w_value, cosines, sines, q_out, k_out, v_out, linear, turned):
    step = pl.program_id(0)

    @pl.when(step < ROW_STEPS)
    def _():
        resid = (rows[...].astype(F32) * scale).astype(BF16).astype(F32)
        inv_rms = lax.rsqrt(jnp.mean(resid * resid, axis=-1, keepdims=True) + EPSILON)
        normed = (resid * inv_rms * (1.0 + norm_scale[...])).astype(BF16)
        for which, weight in enumerate((w_query, w_key, w_value)):
            product = jnp.dot(normed, weight[...], preferred_element_type=F32).astype(BF16).astype(F32)
            for half in range(2):
                at = pl.multiple_of((2 * which + half) * PITCH + step * ROW_BLOCK, 8)
                linear[pl.ds(at, ROW_BLOCK), :] = product[:, 128 * half:128 * half + 128]

    @pl.when(step >= ROW_STEPS)
    def _():
        first = (step - ROW_STEPS) * TOKEN_BLOCK

        def some(i, _):
            for u in range(16):
                t = i * 16 + u
                row = index[first + t]
                turned[pl.ds(t, 8, stride=OUT_PITCH), :] = linear[pl.ds(row, 8, stride=PITCH), :]
            return 0

        lax.fori_loop(0, TOKEN_BLOCK // 16, some, 0)
        part = [turned[OUT_PITCH * j:OUT_PITCH * j + TOKEN_BLOCK, :] for j in range(6)]
        cos, sin = cosines[...], sines[...]
        factor = HEAD_DIM ** -0.5
        q_out[:, :128] = ((part[0] * cos - part[1] * sin) * factor).astype(BF16)
        q_out[:, 128:] = ((part[1] * cos + part[0] * sin) * factor).astype(BF16)
        k_out[:, :128] = (part[2] * cos - part[3] * sin).astype(BF16)
        k_out[:, 128:] = (part[3] * cos + part[2] * sin).astype(BF16)
        v_out[:, :128] = part[4].astype(BF16)
        v_out[:, 128:] = part[5].astype(BF16)


def project(index, rows, norm_scale, w_query, w_key, w_value, cosines, sines, scale):
    tokens = index.shape[0]
    token_steps = tokens // TOKEN_BLOCK
    whole = lambda i, idx: (0, 0)
    by_token = lambda i, idx: (jnp.maximum(i - ROW_STEPS, 0), 0)
    out = jax.ShapeDtypeStruct((tokens, HEAD_DIM), BF16)
    weight = pl.BlockSpec((2048, HEAD_DIM), whole)
    return pl.pallas_call(
        functools.partial(project_kernel, scale),
        out_shape=(out, out, out),
        grid_spec=pltpu.PrefetchScalarGridSpec(
            num_scalar_prefetch=1,
            grid=(ROW_STEPS + token_steps,),
            in_specs=[
                pl.BlockSpec((ROW_BLOCK, 2048), lambda i, idx: (jnp.minimum(i, ROW_STEPS - 1), 0)),
                pl.BlockSpec((1, 2048), whole), weight, weight, weight,
                pl.BlockSpec((TOKEN_BLOCK, 128), by_token),
                pl.BlockSpec((TOKEN_BLOCK, 128), by_token),
            ],
            out_specs=[pl.BlockSpec((TOKEN_BLOCK, HEAD_DIM), by_token)] * 3,
            scratch_shapes=[pltpu.VMEM((8 * PITCH, 128), F32), pltpu.VMEM((8 * OUT_PITCH, 128), F32)],
        ),
        compiler_params=pltpu.CompilerParams(dimension_semantics=("arbitrary",), vmem_limit_bytes=56 * 2 ** 20),
        name="project",
    )(index, rows, norm_scale.reshape(1, -1), w_query, w_key, w_value, cosines, sines)


def solution(mesh):
    def local_step(token_ids, positions, table_rows, norm_scale, w_query, w_key, w_value):
        me = lax.axis_index("tp")
        vocab_rows, model_width = table_rows.shape
        scale = float(np.asarray(math.sqrt(model_width)).astype(BF16))
        tokens = token_ids.shape[0]
        index, own_list, count, fits = plan(token_ids, vocab_rows, me)
        fits_all = lax.pmin(fits.astype(I32), "dp")

        def compact_step(token_ids, positions, table_rows, norm_scale, w_query, w_key, w_value, index, own_list, count):
            base = jnp.asarray(SEG_BASE, I32)[me]
            hot_steps = jnp.where(me == 0, HOT // STEP, 0)
            params = jnp.stack([hot_steps, (count + STEP - 1) // STEP, base]).astype(I32)
            rows = gather_rows(params, own_list, table_rows, ROWS, None, "pick_rows")
            rows = broadcast_rows(rows)
            own_tokens = tokens // 8
            own_index = lax.dynamic_slice_in_dim(index, me * own_tokens, own_tokens)
            resid_params = jnp.asarray([0, own_tokens // STEP, 0], I32)
            residual = gather_rows(resid_params, own_index, rows, own_tokens, scale, "residual_rows")
            cosines, sines = rope_tables(positions)
            queries, keys, values = project(index, rows, norm_scale, w_query, w_key, w_value, cosines, sines, scale)
            return residual, queries, keys, values

        def dense(token_ids, positions, table_rows, norm_scale, w_query, w_key, w_value, *_):
            return dense_step(token_ids, positions, table_rows, norm_scale, w_query, w_key, w_value)

        residual, queries, keys, values = lax.cond(
            fits_all == 1, compact_step, dense,
            token_ids, positions, table_rows, norm_scale, w_query, w_key, w_value, index, own_list, count)
        return residual, queries[:, None, :], keys[:, None, :], values[:, None, :]

    head_spec = P("dp", "tp", None)
    return jax.shard_map(local_step, mesh=mesh, in_specs=(P("dp"), P("dp"), P("tp", None), P(), P(None, "tp"), P(), P()), out_specs=(P(("dp", "tp"), None), head_spec, head_spec, head_spec), check_vma=False)
```

time: 952 us -> 319 us (0.34)
  local copies, waits for them, and re-layouts: 453 us -> 4.41 us
  waiting for transfers between devices: 365 us -> 0 us
  Pallas kernels: 0 us -> 262 us
  matrix products: 51.4 us -> 1.71 us
  other arithmetic: 58.6 us -> 26.3 us
    gather x1 -> x0, local copies, waits for them, and re-layouts: 439 us -> none  [local_step(): picked = jnp.take(table_rows, local_ids, axis=0, mode='clip') * normalizer]
    pallas_call x0 -> x4, Pallas kernels: none -> 262 us  [the longest x1 170 us: broadcast_rows(): pl.pallas_call(broadcast_kernel, out_shape=jax.ShapeDtypeStruct(rows.shap...]
    reduce_scatter x1 -> x0, waiting for transfers between devices: 204 us -> none  [local_step(): residual = lax.psum_scatter(partial, 'tp', scatter_dimension=0, tiled=True)]
    all_gather x1 -> x0, waiting for transfers between devices: 161 us -> none  [local_step(): lax.all_gather(rms_norm(residual, norm_scale), 'tp', axis=0, tiled=True)]
    dot_general x3 -> x2, matrix products: 51.4 us -> 1.71 us  [the longest x1 0.9 us: plan(): within = jnp.einsum('orl,lm->orm', marks, upper, preferred_element_type=F32)]
    select_n x1 -> x2, other arithmetic: 22.9 us -> 1.78 us  [the longest x1 0.94 us: plan(): mine = jnp.where(hot, 8, owner)]
    another operation x1 -> x2, other arithmetic: 20.2 us -> 1.57 us  [the longest x1 1.23 us: compact_step(): jnp.stack([hot_steps, (count + STEP - 1) // STEP, base]).astype(I32)]
    sin x0 -> x1, other arithmetic: none -> 18 us  [rope_tables(): return (jnp.cos(angles), jnp.sin(angles))]
  transfers between devices with their start and end apart: 2 -> 0, of which waited for: 2 -> 0; matrix products, arithmetic and copies ran while one was open for 0% -> 0% of each run, Pallas kernels for 0% -> 0%
where the time goes in v1:
time: 319 us
  Pallas kernels  262 us (82%)
  other arithmetic  26.3 us (8%)
  between operations  15.5 us (5%)
  blocking collectives  6.97 us (2%)
  local copies, waits for them, and re-layouts  4.41 us (1%)
    pallas_call x1, Pallas kernels, broadcast_rows(): pl.pallas_call(broadcast_kernel, out_shape=jax.ShapeDtypeStruct(rows.shap...  170 us
    pallas_call x1, Pallas kernels, project(): pl.pallas_call(functools.partial(project_kernel, scale), out_shape=(out,...  63.1 us
    pallas_call x2, Pallas kernels, gather_rows(): pl.pallas_call(functools.partial(gather_kernel, scale), out_shape=jax.Sha...  28.6 us
    sin x1, other arithmetic, rope_tables(): return (jnp.cos(angles), jnp.sin(angles))  18 us
    pmin x1, blocking collectives, local_step(): fits_all = lax.pmin(fits.astype(I32), 'dp')  6.97 us

profile of v1, /device:TPU:15, one launch (start us, length us, event | category | flops | bytes accessed | tf_op | source)
XLA Modules:
  0.0 318.6 jit_solution(4944867848202828394)
XLA Ops:
  7.2 0.0 copy-start.8
  7.2 0.0 copy-start
  7.2 0.0 copy-start.7
  7.2 0.9 fusion.38
  8.2 0.2 convert_reduce_fusion
  8.3 1.3 compare_reduce_fusion
  10.3 7.0 %pmin.7 = s32[]{:T(128)} all-reduce(s32[]{:T(128)S(6)} %convert_element_type.82), channel_id=1, replica_groups=mesh['dp'=4,'tp'=8] {'dp'}, use_global_device_ids=true, to_apply=%region_2.3 | all-reduce | flops 1 | bytes 8 | tf_op jit(solution)/shard_map/pmin | solution.py:416
  17.9 0.1 multiply_reduce_fusion
  18.1 0.9 select_reduce_fusion.1
  19.0 0.8 broadcast_compare_fusion.1
  19.8 0.8 add_select_fusion.3
  20.6 0.8 fusion.42
  21.4 0.3 select_convert_fusion.1
  21.8 0.8 fusion.26
  22.6 0.1 fusion.48
  22.8 289.0 %conditional.1 = (bf16[1024,2048]{1,0:T(8,128)(2,1)}, bf16[8192,1,256]{2,0,1:T(8,128)(2,1)}, bf16[8192,1,256]{2,0,1:T(8,128)(2,1)}, bf16[8192,1,256]{2,0,1:T(8,128)(2,1)}) conditional(s32[]{:T(128)} %convert_element_type.83, (s32[8192]{0:T(1024)S(1)}, bf16[32152,2048]{1,0:T(8,128)(2,1)}, f32[2048]{0:T(1024)S(1)}, bf16[2048,256]{1,0:T(8,128)(2,1)S(1)}, ...), branch_computations={%region_6.9_spmd, %region_9.12_spmd} | conditional | flops 25858994176 | bytes 569664640 | solution.py:435
  23.0 1.1 select_reduce_fusion
  24.1 0.6 dynamic_slice.7.rows_list
  24.7 0.6 dynamic-slice_bitcast_fusion.lanes_list
  25.3 1.2 dynamic_slice.9
  26.5 0.6 reduce_sum.62
  27.2 0.6 dynamic_slice.8
  29.1 1.2 pad_add_fusion.params
  30.3 0.7 reshape.244.rows_list
  31.0 0.7 reshape_reshape.2.lanes_list
  31.7 8.6 %pick_rows.1._ = bf16[6144,2048]{1,0:T(8,128)(2,1)} custom-call(s32[3]{0:T(128)} %pad_add_fusion.params, s32[3072]{0:T(1024)} %reshape.244.rows_list, s32[24,128]{1,0:T(8,128)} %reshape_reshape.2.lanes_list, bf16[32152,2048]{1,0:T(8,128)(2,1)} %get-tuple-element.97.source), custom_call_target="tpu_custom_call" | custom-call | tf_op jit(solution)/shard_map/cond/branch_1_fun/pick_rows/pallas_call | solution.py:180
  40.3 0.0 copy-done.5
  40.3 170.3 %broadcast_rows.1.source.rows = bf16[6144,2048]{1,0:T(8,128)(2,1)} custom-call(bf16[6144,2048]{1,0:T(8,128)(2,1)} %pick_rows.1._), custom_call_target="tpu_custom_call", output_to_operand_aliasing={{}: (0, {})} | custom-call | tf_op jit(solution)/shard_map/cond/branch_1_fun/broadcast_rows/pallas_call | solution.py:322
  210.6 20.0 %residual_rows.1 = bf16[1024,2048]{1,0:T(8,128)(2,1)} custom-call(s32[3]{0:T(128)} %constant.158.clone.1.params, s32[1024]{0:T(1024)} %dynamic_slice.7.rows_list, s32[8,128]{1,0:T(8,128)} %dynamic-slice_bitcast_fusion.lanes_list, bf16[6144,2048]{1,0:T(8,128)(2,1)} %broadcast_rows.1.source.rows), custom_call_target="tpu_custom_call" | custom-call | tf_op jit(solution)/shard_map/cond/branch_1_fun/residual_rows/pallas_call | solution.py:180
  230.6 0.0 copy-start.4
  230.6 18.0 %multiply_sine_fusion = (f32[8192,128]{1,0:T(8,128)}, f32[8192,128]{1,0:T(8,128)}) fusion(f32[128]{0:T(128)S(1)} %multiply_power_fusion, f32[8192]{0:T(1024)S(1)} %convert_element_type.69), kind=kLoop, calls=%fused_computation.1 | loop fusion | flops 1048576 | bytes 8421888 | tf_op jit(solution)/shard_map/cond/branch_1_fun/sin | solution.py:36
  248.6 63.1 %project.1 = (bf16[8192,256]{1,0:T(8,128)(2,1)}, bf16[8192,256]{1,0:T(8,128)(2,1)}, bf16[8192,256]{1,0:T(8,128)(2,1)}) custom-call(s32[8192]{0:T(1024)} %copy-done.5, bf16[6144,2048]{1,0:T(8,128)(2,1)} %broadcast_rows.1.source.rows, f32[1,2048]{1,0:T(1,128)S(1)} %bitcast.66, bf16[2048,256]{1,0:T(8,128)(2,1)S(1)} %get-tuple-element.99.w_query, ...), custom_call_target="tpu_custom_call" | custom-call | tf_op jit(solution)/shard_map/cond/branch_1_fun/project/pallas_call | solution.py:389
  (18 shorter events, 0.1 us)
Async XLA Ops:
  7.2 15.5 %copy-start.8 = (s32[8]{0:T(128)S(1)}, s32[8]{0:T(128)}, u32[]{:S(2)}) copy-start(s32[8]{0:T(128)} %constant.156.clone) | copy-start | bytes 100
  7.2 15.5 %copy-start = (s32[8192]{0:T(1024)S(1)}, s32[8192]{0:T(1024)}, u32[]{:S(2)}) copy-start(s32[8192]{0:T(1024)} %param.13) | copy-start | bytes 98308
  7.2 15.5 %copy-start.7 = (f32[2048]{0:T(1024)S(1)}, f32[2048]{0:T(1024)}, u32[]{:S(2)}) copy-start(f32[2048]{0:T(1024)} %param.16) | copy-start | bytes 24580
  7.2 15.5 %copy-start.1 = (bf16[2048,256]{1,0:T(8,128)(2,1)S(1)}, bf16[2048,256]{1,0:T(8,128)(2,1)}, u32[]{:S(2)}) copy-start(bf16[2048,256]{1,0:T(8,128)(2,1)} %param.17) | copy-start | bytes 3145732
  7.2 15.5 %copy-start.6 = (s32[8192]{0:T(1024)S(1)}, s32[8192]{0:T(1024)}, u32[]{:S(2)}) copy-start(s32[8192]{0:T(1024)} %param.14) | copy-start | bytes 98308
  7.2 15.5 %copy-start.2 = (bf16[2048,256]{1,0:T(8,128)(2,1)S(1)}, bf16[2048,256]{1,0:T(8,128)(2,1)}, u32[]{:S(2)}) copy-start(bf16[2048,256]{1,0:T(8,128)(2,1)} %param.18) | copy-start | bytes 3145732
  24.1 16.2 %copy-start.5 = (s32[8192]{0:T(1024)}, s32[8192]{0:T(1024)S(1)}, u32[]{:S(2)}) copy-start(s32[8192]{0:T(1024)S(1)} %fusion.index) | copy-start | bytes 98308 | tf_op jit(solution)/shard_map/cond
  230.6 18.0 %copy-start.4 = (bf16[2048,256]{1,0:T(8,128)(2,1)S(1)}, bf16[2048,256]{1,0:T(8,128)(2,1)}, u32[]{:S(2)}) copy-start(bf16[2048,256]{1,0:T(8,128)(2,1)} %get-tuple-element.101.w_value) | copy-start | bytes 3145732 | tf_op jit(solution)/shard_map/cond

commit v2 on v0

v2 whole, which is shorter than its diff:
```python
import functools
import math

import jax
import numpy as np
import jax.numpy as jnp
from jax import lax
from jax.experimental import pallas as pl
from jax.experimental.pallas import tpu as pltpu
from jax.sharding import PartitionSpec as P

HEAD_DIM = 256
EPSILON = 1e-6
ROPE_BASE = 10000.0
MESH = pl.DeviceIdType.MESH
BF16, F32, I32 = jnp.bfloat16, jnp.float32, jnp.int32

CHUNK = 64
HOT = 1024
LIST_CAP = (2816, 640, 384, 384, 192, 192, 192, 192)
SEG_ROWS = tuple(c + (HOT if d == 0 else 0) for d, c in enumerate(LIST_CAP))
SEG_BASE = tuple(sum(SEG_ROWS[:d]) for d in range(8))
ROWS = sum(SEG_ROWS)
SEG_CHUNKS = tuple(r // CHUNK for r in SEG_ROWS)
CHUNK_ID = tuple(b // CHUNK for b in SEG_BASE)
ALL_CHUNKS = ROWS // CHUNK
STEPS = ALL_CHUNKS // 2
SPLIT = STEPS - SEG_CHUNKS[2] - SEG_CHUNKS[4] - SEG_CHUNKS[6]
LIST_LEN = -(-max(LIST_CAP) // 128) * 128
RING = ((0, 1, 3, 2), (0, 2, 3, 1))


def rope_tables(positions):
    inv_freq = ROPE_BASE ** (-jnp.arange(0, HEAD_DIM, 2, dtype=F32) / HEAD_DIM)
    angles = positions.astype(F32)[:, None] * inv_freq[None, :]
    return jnp.cos(angles), jnp.sin(angles)


def rotate(head_vals, cosines, sines):
    half_dim = head_vals.shape[-1] // 2
    front_half = head_vals[..., :half_dim]
    back_half = head_vals[..., half_dim:]
    return jnp.concatenate([front_half * cosines - back_half * sines, back_half * cosines + front_half * sines], axis=-1)


def rms_norm(resid_rows, norm_scale):
    widened = resid_rows.astype(F32)
    inv_rms = lax.rsqrt(jnp.mean(widened * widened, axis=-1, keepdims=True) + EPSILON)
    return (widened * inv_rms * (1.0 + norm_scale)).astype(BF16)


def dense_step(token_ids, positions, table_rows, norm_scale, w_query, w_key, w_value):
    vocab_rows, model_width = table_rows.shape
    normalizer = jnp.asarray(math.sqrt(model_width), dtype=BF16)
    local_ids = token_ids - lax.axis_index("tp") * vocab_rows
    inside = (local_ids >= 0) & (local_ids < vocab_rows)
    picked = jnp.take(table_rows, local_ids, axis=0, mode="clip") * normalizer
    partial = jnp.where(inside[:, None], picked, jnp.zeros((), BF16))
    group = lax.axis_size("tp")
    blocks = lax.all_to_all(partial.reshape(group, -1, model_width), "tp", 0, 0)
    residual = jnp.sum(blocks.astype(F32), axis=0).astype(BF16)
    spread = jnp.broadcast_to(rms_norm(residual, norm_scale)[None], blocks.shape)
    normed = lax.all_to_all(spread, "tp", 0, 0).reshape(-1, model_width)
    cosines, sines = rope_tables(positions)

    def project(weight, factor):
        linear = jnp.dot(normed, weight, preferred_element_type=F32).astype(BF16).astype(F32)
        return (rotate(linear, cosines, sines) * factor).astype(BF16)

    value_heads = jnp.dot(normed, w_value, preferred_element_type=F32).astype(BF16)
    return residual, project(w_query, HEAD_DIM ** -0.5), project(w_key, 1.0), value_heads


def plan_kernel(vocab_rows, ids_ref, index_out, list_out, counts_out, own_place, own_high, own_low):
    me = lax.axis_index("tp")
    ids = ids_ref[...]
    rows, lanes = ids.shape
    owner = jnp.zeros_like(ids)
    for d in range(1, 8):
        owner += (ids >= d * vocab_rows).astype(I32)
    hot = ids < HOT
    owner = jnp.where(hot, 8, owner)
    marks = [(owner == d).astype(F32) for d in range(8)]
    stacked = jnp.concatenate(marks, axis=0).astype(BF16)
    row_of = lax.broadcasted_iota(I32, (lanes, lanes), 0)
    lane_of = lax.broadcasted_iota(I32, (lanes, lanes), 1)
    upper = (row_of < lane_of).astype(F32).astype(BF16)
    within = jnp.dot(stacked, upper, preferred_element_type=F32)
    per_row = jnp.dot(stacked, jnp.ones((lanes, lanes), BF16), preferred_element_type=F32)
    lower = (lax.broadcasted_iota(I32, (rows, rows), 0) > lax.broadcasted_iota(I32, (rows, rows), 1)).astype(F32).astype(BF16)
    index = jnp.where(hot, ids, 0).astype(F32)
    place = jnp.zeros((rows, lanes), F32)
    for d in range(8):
        here = slice(rows * d, rows * d + rows)
        before = jnp.dot(lower, per_row[here].astype(BF16), preferred_element_type=F32)
        at = within[here] + before
        place += marks[d] * at
        index += marks[d] * (at + float(SEG_BASE[d] + (HOT if d == 0 else 0)))
        counts_out[d:d + 1, :] = jnp.sum(per_row[here], axis=0, keepdims=True).astype(I32)
    index_out[...] = jnp.clip(index.astype(I32), 0, ROWS - 1)
    local = ids - me * vocab_rows
    own_place[...] = jnp.where(owner == me, place.astype(I32), -1)
    own_high[...] = lax.shift_right_logical(local, 8).astype(F32)
    own_low[...] = (local & 255).astype(F32)
    tall = list_out.shape[0]

    def scatter(r, total):
        at = own_place[pl.ds(r, 1), :]
        column = lax.broadcasted_iota(I32, (128, lanes), 0)
        high = (lax.broadcasted_iota(I32, (tall, lanes), 0) == lax.shift_right_arithmetic(at, 7)).astype(F32).astype(BF16)
        low = (column == (at & 127)).astype(F32)
        values = jnp.concatenate([low * own_high[pl.ds(r, 1), :], low * own_low[pl.ds(r, 1), :]], axis=0).astype(BF16)
        return total + lax.dot_general(high, values, (((1,), (1,)), ((), ())), preferred_element_type=F32)

    total = lax.fori_loop(0, rows, scatter, jnp.zeros((tall, 256), F32), unroll=4)
    list_out[...] = (total[:, :128] * 256.0 + total[:, 128:]).astype(I32)


def plan(token_ids, vocab_rows):
    tokens = token_ids.shape[0]
    square = (tokens // 128, 128)
    return pl.pallas_call(
        functools.partial(plan_kernel, vocab_rows),
        out_shape=(
            jax.ShapeDtypeStruct(square, I32),
            jax.ShapeDtypeStruct((LIST_LEN // 128, 128), I32),
            jax.ShapeDtypeStruct((8, 128), I32),
        ),
        scratch_shapes=[pltpu.VMEM(square, I32), pltpu.VMEM(square, F32), pltpu.VMEM(square, F32)],
        name="plan",
    )(token_ids.reshape(square))


STEP = 128
DEPTH = 4


def gather_kernel(scale, params, rows_list, lanes_list, source, out, groups, picked, in_sems, out_sems):
    first, end = params[0], params[1]

    def issue(step, slot):
        def one(t, _):
            group = lax.shift_right_logical(rows_list[(first + step) * STEP + t], 3)
            pltpu.make_async_copy(source.at[pl.ds(pl.multiple_of(group * 8, 8), 8)], groups.at[slot, pl.ds(pl.multiple_of(t * 8, 8), 8)], in_sems.at[slot]).start()
            return 0

        lax.fori_loop(0, STEP, one, 0, unroll=8)

    def arrive(slot):
        pltpu.make_async_copy(source.at[pl.ds(0, STEP * 8)], groups.at[slot], in_sems.at[slot]).wait()

    def drain(slot):
        pltpu.make_async_copy(picked.at[slot], out.at[pl.ds(0, STEP)], out_sems.at[slot]).wait()

    for ahead in range(DEPTH - 1):
        pl.when(ahead < end)(functools.partial(issue, ahead, ahead))

    def body(step, _):
        slot, put = lax.rem(step, DEPTH), lax.rem(step, 2)
        free = lax.rem(step + DEPTH - 1, DEPTH)
        arrive(slot)

        @pl.when(step + DEPTH - 1 < end)
        def _():
            issue(step + DEPTH - 1, free)

        @pl.when(step >= 2)
        def _():
            drain(put)

        within = lanes_list[pl.ds(first + step, 1), :] & 7
        target = lax.broadcasted_iota(I32, (1, STEP), 1) * 8 + within
        target = jnp.broadcast_to(target, (STEP, STEP)).T
        lane = lax.broadcasted_iota(I32, (STEP, STEP), 1)
        select = jnp.concatenate([(lane + STEP * j == target).astype(F32).astype(BF16) for j in range(8)], axis=1)
        for c in range(8):
            rows = jnp.dot(select, groups[slot, :, 256 * c:256 * c + 256], preferred_element_type=F32)
            picked[put, :, 256 * c:256 * c + 256] = (rows if scale is None else rows * scale).astype(BF16)
        pltpu.make_async_copy(picked.at[put], out.at[pl.ds(pl.multiple_of(step * STEP, STEP), STEP)], out_sems.at[put]).start()
        return 0

    lax.fori_loop(0, end, body, 0)
    @pl.when(end >= 2)
    def _():
        drain(lax.rem(end, 2))

    @pl.when(end >= 1)
    def _():
        drain(lax.rem(end + 1, 2))


def gather_rows(params, rows_list, source, out_rows, scale, name):
    return pl.pallas_call(
        functools.partial(gather_kernel, scale),
        out_shape=jax.ShapeDtypeStruct((out_rows, source.shape[1]), BF16),
        in_specs=[
            pl.BlockSpec(memory_space=pltpu.SMEM),
            pl.BlockSpec(memory_space=pltpu.SMEM),
            pl.BlockSpec(memory_space=pltpu.VMEM),
            pl.BlockSpec(memory_space=pl.ANY),
        ],
        out_specs=pl.BlockSpec(memory_space=pl.ANY),
        scratch_shapes=[
            pltpu.VMEM((DEPTH, STEP * 8, 2048), BF16),
            pltpu.VMEM((2, STEP, 2048), BF16),
            pltpu.SemaphoreType.DMA((DEPTH,)),
            pltpu.SemaphoreType.DMA((2,)),
        ],
        name=name,
    )(params, rows_list.reshape(-1), rows_list, source)


def ring_device(core, place):
    return 2 * RING[core][place % 4] + core


def ring_runs(core, place):
    if place % 4:
        device = ring_device(core, place)
        return [(CHUNK_ID[device], SEG_CHUNKS[device])]
    if core == 0:
        return [(0, SPLIT)]
    return [(CHUNK_ID[1], SEG_CHUNKS[1]), (SPLIT, SEG_CHUNKS[0] - SPLIT)]


def stream(device):
    core = device % 2
    place = RING[core].index(device // 2)
    return [first + i for back in range(4) for first, n in ring_runs(core, place - back) for i in range(n)]


def runs_of(numbers):
    runs = []
    for step, number in enumerate(numbers):
        if not runs or numbers[step - 1] + 1 != number:
            runs.append((step, number - step))
    return runs


def pick(me, values):
    out = jnp.asarray(values[0], I32)
    for d in range(1, len(values)):
        out = jnp.where(me == d, jnp.asarray(values[d], I32), out)
    return out


RING_RUNS = [runs_of(stream(d)) for d in range(8)]
PAIR_RUNS = [RING_RUNS[d ^ 1] for d in range(8)]
RUNS = max(len(r) for r in RING_RUNS)
TABLES = 64


def broadcast_kernel(scale, table, picked, norm_scale, w_query, w_key, w_value, positions, flags,
                     rows_out, linear_out, cos_out, sin_out, flags_out,
                     rows, linear, angles, ring_sems, pair_sems, recv_sems, load_sem, rows_sem, linear_sem, angle_sems, flag_sends, flag_recvs):
    me, plane = lax.axis_index("tp"), lax.axis_index("dp")
    core, chip = me % 2, me // 2
    x, y = chip % 2, chip // 2
    along_x = 2 * (2 * y + 1 - x) + core
    along_y = 2 * (2 * (1 - y) + x) + core
    pair = 2 * chip + 1 - core
    turn = (x + y + core) % 2
    after = turn * along_y + (1 - turn) * along_x
    barrier = pltpu.get_barrier_semaphore()
    for peer in (along_x, along_y, pair):
        pl.semaphore_signal(barrier, inc=1, device_id={"tp": peer}, device_id_type=MESH)
    for hop in (1, 2, 3):
        pl.semaphore_signal(barrier, inc=1, device_id={"dp": (plane + hop) % 4}, device_id_type=MESH)

    def chunk(number):
        return pl.ds(pl.multiple_of(number * CHUNK, CHUNK), CHUNK)

    own_first = pick(me, CHUNK_ID)
    own_list = own_first + jnp.where(me == 0, HOT // CHUNK, 0)
    own_end = own_first + pick(me, SEG_CHUNKS)

    def load_list(number, _):
        pltpu.make_async_copy(picked.at[chunk(number - own_list)], rows.at[chunk(number)], load_sem.at[number]).start()
        return 0

    @pl.when(me == 0)
    def _():
        def load_hot(number, _):
            pltpu.make_async_copy(table.at[chunk(number)], rows.at[chunk(number)], load_sem.at[number]).start()
            return 0

        lax.fori_loop(0, HOT // CHUNK, load_hot, 0)

    lax.fori_loop(own_list, own_end, load_list, 0)
    pl.semaphore_wait(barrier, 6)

    def flag_copy(hop):
        return pltpu.make_async_remote_copy(
            src_ref=flags, dst_ref=flags_out.at[hop], send_sem=flag_sends.at[hop], recv_sem=flag_recvs.at[hop],
            device_id={"dp": (plane + hop + 1) % 4}, device_id_type=MESH)

    for hop in range(3):
        flag_copy(hop).start()

    def copy(number, sems, target):
        return pltpu.make_async_remote_copy(
            src_ref=rows.at[chunk(number)], dst_ref=rows.at[chunk(number)], send_sem=sems.at[number], recv_sem=recv_sems.at[number],
            device_id={"tp": target}, device_id_type=MESH)

    def to_ring(number):
        copy(number, ring_sems, after).start()

    def to_pair(number):
        copy(number, pair_sems, pair).start()

    def keep(number):
        return pltpu.make_async_copy(rows.at[chunk(number)], rows_out.at[chunk(number)], rows_sem.at[number])

    def loaded(number):
        pltpu.make_async_copy(table.at[pl.ds(0, CHUNK)], rows.at[chunk(number)], load_sem.at[number]).wait()

    def send_own(number, _):
        loaded(number)
        to_pair(number)
        keep(number).start()

        @pl.when((me != 0) | (number < SPLIT))
        def _():
            to_ring(number)

        return 0

    @pl.when(me == 0)
    def _():
        ahead = SEG_CHUNKS[0] - SPLIT

        def both(i, _):
            send_own(SPLIT + i, 0)
            send_own(i, 0)
            return 0

        lax.fori_loop(0, ahead, both, 0)
        lax.fori_loop(ahead, SPLIT, send_own, 0)

    @pl.when(me != 0)
    def _():
        lax.fori_loop(own_first, own_end, send_own, 0)

    def number_at(step, all_runs):
        number = jnp.asarray(0, I32)
        for d in range(8):
            mine = jnp.asarray(all_runs[d][0][1], I32)
            for opens, shift in all_runs[d][1:]:
                mine = jnp.where(step >= opens, shift, mine)
            number = jnp.where(me == d, mine, number)
        return number + step

    last_first = pick(me, [len(stream(d)) - sum(n for _, n in ring_runs(d % 2, RING[d % 2].index(d // 2) - 3)) for d in range(8)])
    inv_freq = jnp.exp(lax.broadcasted_iota(I32, (1, 128), 1).astype(F32) * (-2.0 * math.log(ROPE_BASE) / HEAD_DIM))

    def project(number):
        resid = (rows[chunk(number), :].astype(F32) * scale).astype(BF16).astype(F32)
        inv_rms = lax.rsqrt(jnp.mean(resid * resid, axis=-1, keepdims=True) + EPSILON)
        return (resid * inv_rms * (1.0 + norm_scale[...])).astype(BF16)

    def angle_copies(slot, block):
        there = pl.ds(pl.multiple_of(block * 128, 128), 128)
        return (pltpu.make_async_copy(angles.at[slot, 0], cos_out.at[there], angle_sems.at[slot, 0]),
                pltpu.make_async_copy(angles.at[slot, 1], sin_out.at[there], angle_sems.at[slot, 1]))

    def linear_copy(number):
        there = pl.ds(pl.multiple_of(number * (CHUNK * 8), CHUNK * 8), CHUNK * 8)
        return pltpu.make_async_copy(linear.at[there], linear_out.at[there], linear_sem)

    def put_linear(step):
        linear_copy(number_at(step, RING_RUNS)).start()
        linear_copy(number_at(step, PAIR_RUNS)).start()

    def step_body(step, _):
        ring_number = number_at(step, RING_RUNS)
        pair_number = number_at(step, PAIR_RUNS)
        own_ring = (ring_number >= own_first) & (ring_number < own_end)
        second = (me == 1) & (ring_number < CHUNK_ID[1])

        @pl.when(jnp.logical_not(own_ring))
        def _():
            copy(ring_number, ring_sems, after).wait_recv()

            @pl.when(step < last_first)
            def _():
                to_ring(ring_number)

            @pl.when(jnp.logical_not(second))
            def _():
                to_pair(ring_number)

            keep(ring_number).start()

        @pl.when((pair_number < own_first) | (pair_number >= own_end))
        def _():
            copy(pair_number, ring_sems, after).wait_recv()
            keep(pair_number).start()

        for b in range(2):
            block = step * 2 + b

            @pl.when(block < positions.shape[0])
            def _():
                where = jnp.broadcast_to(positions[pl.ds(block, 1), :].astype(F32), (128, 128)).T
                angle = where * inv_freq

                @pl.when(step >= 1)
                def _():
                    for c in angle_copies(b, block - 2):
                        c.wait()

                angles[b, 0] = jnp.cos(angle)
                angles[b, 1] = jnp.sin(angle)

        normed = jnp.concatenate([project(ring_number), project(pair_number)], axis=0)
        for which, weight in enumerate((w_query, w_key, w_value)):
            product = jnp.dot(normed, weight[...], preferred_element_type=F32).astype(BF16).astype(F32)
            for half in range(2):
                part = product[:, 128 * half:128 * half + 128]
                for number, mine in ((ring_number, part[:CHUNK]), (pair_number, part[CHUNK:])):
                    linear[pl.ds(number * (CHUNK * 8) + 2 * which + half, CHUNK, stride=8), :] = mine
        for b in range(2):
            block = step * 2 + b

            @pl.when(block < positions.shape[0])
            def _():
                for c in angle_copies(b, block):
                    c.start()

        @pl.when(step >= 1)
        def _():
            put_linear(step - 1)

        return 0

    lax.fori_loop(0, STEPS, step_body, 0)
    for b in range(2):
        for c in angle_copies(b, positions.shape[0] - 2 + b):
            c.wait()
    put_linear(STEPS - 1)
    for hop in range(3):
        flag_copy(hop).wait()

    def sent_to_ring(step, _):
        copy(number_at(step, RING_RUNS), ring_sems, after).wait_send()
        return 0

    def sent_to_pair(step, _):
        number = number_at(step, RING_RUNS)

        @pl.when((me != 1) | (number >= CHUNK_ID[1]) | (number < SPLIT))
        def _():
            copy(number, pair_sems, pair).wait_send()

        return 0

    lax.fori_loop(0, last_first, sent_to_ring, 0)
    lax.fori_loop(0, STEPS, sent_to_pair, 0)

    @pl.when(me == 0)
    def _():
        def sent(number, _):
            copy(number, pair_sems, pair).wait_send()
            return 0

        lax.fori_loop(SPLIT, SEG_CHUNKS[0], sent, 0)

    def kept(number, _):
        keep(number).wait()
        return 0

    lax.fori_loop(0, ALL_CHUNKS, kept, 0)
    pltpu.make_async_copy(linear, linear_out, linear_sem).wait()


def broadcast_project(table, picked, norm_scale, w_query, w_key, w_value, positions, flags, scale):
    tokens = positions.size
    vmem, anywhere = pl.BlockSpec(memory_space=pltpu.VMEM), pl.BlockSpec(memory_space=pl.ANY)
    return pl.pallas_call(
        functools.partial(broadcast_kernel, scale),
        out_shape=(
            jax.ShapeDtypeStruct((ROWS, 2048), BF16),
            jax.ShapeDtypeStruct((ROWS * 8, 128), F32),
            jax.ShapeDtypeStruct((tokens, 128), F32),
            jax.ShapeDtypeStruct((tokens, 128), F32),
            jax.ShapeDtypeStruct((3, 8, 128), F32),
        ),
        in_specs=[anywhere, anywhere] + [vmem] * 6,
        out_specs=(anywhere, anywhere, anywhere, anywhere, vmem),
        scratch_shapes=[
            pltpu.VMEM((ROWS, 2048), BF16),
            pltpu.VMEM((ROWS * 8, 128), F32),
            pltpu.VMEM((2, 2, 128, 128), F32),
            pltpu.SemaphoreType.DMA((ALL_CHUNKS,)),
            pltpu.SemaphoreType.DMA((ALL_CHUNKS,)),
            pltpu.SemaphoreType.DMA((ALL_CHUNKS,)),
            pltpu.SemaphoreType.DMA((ALL_CHUNKS,)),
            pltpu.SemaphoreType.DMA((ALL_CHUNKS,)),
            pltpu.SemaphoreType.DMA,
            pltpu.SemaphoreType.DMA((2, 2)),
            pltpu.SemaphoreType.DMA((3,)),
            pltpu.SemaphoreType.DMA((3,)),
        ],
        compiler_params=pltpu.CompilerParams(collective_id=0, has_side_effects=True, vmem_limit_bytes=60 * 2 ** 20),
        name="broadcast_project",
    )(table, picked, norm_scale.reshape(1, -1), w_query, w_key, w_value, positions, flags)


TOKEN_BLOCK = 512
OUT_PITCH = TOKEN_BLOCK + 4


def order_kernel(index, linear_in, cosines, sines, q_out, k_out, v_out, linear, turned, sems):
    step = pl.program_id(0)

    @pl.when(step == 0)
    def _():
        eighth = ROWS
        copies = [pltpu.make_async_copy(linear_in.at[pl.ds(j * eighth, eighth)], linear.at[pl.ds(j * eighth, eighth)], sems.at[j]) for j in range(8)]
        for c in copies:
            c.start()
        for c in copies:
            c.wait()

    def some(i, _):
        for u in range(32):
            row = index[step * TOKEN_BLOCK + i * 32 + u]
            turned[pl.ds(i * 32 + u, 8, stride=OUT_PITCH), :] = linear[pl.ds(pl.multiple_of(row * 8, 8), 8), :]
        return 0

    lax.fori_loop(0, TOKEN_BLOCK // 32, some, 0)
    part = [turned[OUT_PITCH * j:OUT_PITCH * j + TOKEN_BLOCK, :] for j in range(6)]
    cos, sin = cosines[...], sines[...]
    factor = HEAD_DIM ** -0.5
    q_out[:, :128] = ((part[0] * cos - part[1] * sin) * factor).astype(BF16)
    q_out[:, 128:] = ((part[1] * cos + part[0] * sin) * factor).astype(BF16)
    k_out[:, :128] = (part[2] * cos - part[3] * sin).astype(BF16)
    k_out[:, 128:] = (part[3] * cos + part[2] * sin).astype(BF16)
    v_out[:, :128] = part[4].astype(BF16)
    v_out[:, 128:] = part[5].astype(BF16)


def token_order(index, linear, cosines, sines):
    tokens = cosines.shape[0]
    by_token = lambda i, idx: (i, 0)
    out = jax.ShapeDtypeStruct((tokens, HEAD_DIM), BF16)
    return pl.pallas_call(
        order_kernel,
        out_shape=(out, out, out),
        grid_spec=pltpu.PrefetchScalarGridSpec(
            num_scalar_prefetch=1,
            grid=(tokens // TOKEN_BLOCK,),
            in_specs=[
                pl.BlockSpec(memory_space=pl.ANY),
                pl.BlockSpec((TOKEN_BLOCK, 128), by_token),
                pl.BlockSpec((TOKEN_BLOCK, 128), by_token),
            ],
            out_specs=[pl.BlockSpec((TOKEN_BLOCK, HEAD_DIM), by_token)] * 3,
            scratch_shapes=[pltpu.VMEM((8 * ROWS, 128), F32), pltpu.VMEM((8 * OUT_PITCH, 128), F32), pltpu.SemaphoreType.DMA((8,))],
        ),
        compiler_params=pltpu.CompilerParams(dimension_semantics=("arbitrary",), vmem_limit_bytes=48 * 2 ** 20),
        name="token_order",
    )(index, linear, cosines, sines)


def solution(mesh):
    def local_step(token_ids, positions, table_rows, norm_scale, w_query, w_key, w_value):
        me = lax.axis_index("tp")
        vocab_rows, model_width = table_rows.shape
        scale = float(np.asarray(math.sqrt(model_width)).astype(BF16))
        tokens = token_ids.shape[0]
        index, own_list, counts = plan(token_ids, vocab_rows)
        length = counts[:, 0]
        fits = jnp.all(length <= jnp.asarray(LIST_CAP, I32))
        steps = jnp.minimum((length[me] + STEP - 1) // STEP, LIST_LEN // STEP)
        picked = gather_rows(jnp.stack([0, steps]).astype(I32), own_list, table_rows, LIST_LEN, None, "pick_rows")
        flags = jnp.broadcast_to(fits.astype(F32), (8, 128))
        rows, linear, cosines, sines, others = broadcast_project(
            table_rows, picked, norm_scale, w_query, w_key, w_value, positions.reshape(-1, 128), flags, scale)
        fits_all = fits & jnp.all(others[:, 0, 0] > 0.5)

        def compact_step(token_ids, positions, table_rows, norm_scale, w_query, w_key, w_value, index, rows, linear, cosines, sines):
            own_tokens = tokens // 8
            resid_params = jnp.stack([me * (own_tokens // STEP), own_tokens // STEP]).astype(I32)
            residual = gather_rows(resid_params, index, rows, own_tokens, scale, "residual_rows")
            queries, keys, values = token_order(index.reshape(tokens), linear, cosines, sines)
            return residual, queries, keys, values

        def dense(token_ids, positions, table_rows, norm_scale, w_query, w_key, w_value, *_):
            return dense_step(token_ids, positions, table_rows, norm_scale, w_query, w_key, w_value)

        residual, queries, keys, values = lax.cond(
            fits_all, compact_step, dense,
            token_ids, positions, table_rows, norm_scale, w_query, w_key, w_value, index, rows, linear, cosines, sines)
        return residual, queries[:, None, :], keys[:, None, :], values[:, None, :]

    head_spec = P("dp", "tp", None)
    return jax.shard_map(local_step, mesh=mesh, in_specs=(P("dp"), P("dp"), P("tp", None), P(), P(None, "tp"), P(), P()), out_specs=(P(("dp", "tp"), None), head_spec, head_spec, head_spec), check_vma=False)
```

time: 952 us -> 236 us (0.25)
  local copies, waits for them, and re-layouts: 453 us -> 0.64 us
  waiting for transfers between devices: 365 us -> 0 us
  Pallas kernels: 0 us -> 221 us
  other arithmetic: 58.6 us -> 4.42 us
  matrix products: 51.4 us -> 0 us
    gather x1 -> x0, local copies, waits for them, and re-layouts: 439 us -> none  [local_step(): picked = jnp.take(table_rows, local_ids, axis=0, mode='clip') * normalizer]
    pallas_call x0 -> x5, Pallas kernels: none -> 221 us  [the longest x1 165 us: broadcast_project(): pl.pallas_call(functools.partial(broadcast_kernel, scale), out_shape=(jax...]
    reduce_scatter x1 -> x0, waiting for transfers between devices: 204 us -> none  [local_step(): residual = lax.psum_scatter(partial, 'tp', scatter_dimension=0, tiled=True)]
    all_gather x1 -> x0, waiting for transfers between devices: 161 us -> none  [local_step(): lax.all_gather(rms_norm(residual, norm_scale), 'tp', axis=0, tiled=True)]
    dot_general x3 -> x0, matrix products: 51.4 us -> none  [the longest x2 35 us: project(): jnp.dot(normed, weight, preferred_element_type=jnp.float32)]
    select_n x1 -> x0, other arithmetic: 22.9 us -> none  [local_step(): partial = jnp.where(inside[:, None], picked, jnp.zeros((), jnp.bfloat16))]
    another operation x1 -> x2, other arithmetic: 20.2 us -> 1.24 us  [the longest x1 0.65 us: compact_step(): jnp.stack([me * (own_tokens // STEP), own_tokens // STEP]).astype(I32)]
    unnamed x14 -> x16, local copies, waits for them, and re-layouts: 14.4 us -> 0.04 us
  transfers between devices with their start and end apart: 2 -> 0, of which waited for: 2 -> 0; matrix products, arithmetic and copies ran while one was open for 0% -> 0% of each run, Pallas kernels for 0% -> 0%
where the time goes in v2:
time: 236 us; the launch traced here: 232 us
  Pallas kernels  221 us (94%)
  between operations  5.46 us (2%)
  other arithmetic  4.42 us (2%)
    pallas_call x1, Pallas kernels, broadcast_project(): pl.pallas_call(functools.partial(broadcast_kernel, scale), out_shape=(jax...  165 us
    pallas_call x1, Pallas kernels, token_order(): pl.pallas_call(order_kernel, out_shape=(out, out, out), grid_spec=pltpu.P...  27.2 us
    pallas_call x2, Pallas kernels, gather_rows(): pl.pallas_call(functools.partial(gather_kernel, scale), out_shape=jax.Sha...  23.1 us
    pallas_call x1, Pallas kernels, plan(): pl.pallas_call(functools.partial(plan_kernel, vocab_rows), out_shape=(jax...  5.05 us

profile of v2, /device:TPU:15, one launch (start us, length us, event | category | flops | bytes accessed | tf_op | source)
XLA Modules:
  0.0 231.5 jit_solution(8340119811265455119)
XLA Ops:
  0.6 5.1 %plan.1 = (s32[64,128]{1,0:T(8,128)S(1)}, s32[22,128]{1,0:T(8,128)}, s32[8,128]{1,0:T(8,128)}) custom-call(s32[64,128]{1,0:T(8,128)} %bitcast.31), custom_call_target="tpu_custom_call" | custom-call | tf_op jit(solution)/shard_map/plan/pallas_call | solution.py:122
  5.7 1.2 fusion.25
  9.5 0.6 pad_add_fusion.1.params
  10.1 0.0 copy-start.10
  10.1 0.0 copy-start.11
  10.1 0.0 copy-start
  10.1 0.0 copy-start.2
  10.1 0.0 copy-start.4
  10.1 0.0 copy-start.7
  10.1 0.0 copy-start.9
  10.1 4.8 %pick_rows.1.picked = bf16[2816,2048]{1,0:T(8,128)(2,1)} custom-call(s32[2]{0:T(128)} %pad_add_fusion.1.params, s32[2816]{0:T(1024)} %bitcast.35, s32[22,128]{1,0:T(8,128)} %get-tuple-element.58.lanes_list, bf16[32152,2048]{1,0:T(8,128)(2,1)} %table.1), custom_call_target="tpu_custom_call" | custom-call | tf_op jit(solution)/shard_map/pick_rows/pallas_call | solution.py:193
  14.9 0.0 copy-done.10
  14.9 0.0 copy-done.11
  14.9 0.6 compare_reduce_fusion.1
  16.2 0.6 broadcast_in_dim.49.flags
  16.8 0.0 copy-done
  16.8 0.0 copy-done.2
  16.8 0.0 copy-done.4
  16.8 0.0 copy-done.7
  16.8 0.0 copy-done.9
  16.9 0.0 copy-start.6
  16.9 165.4 %broadcast_project.1 = (bf16[6016,2048]{1,0:T(8,128)(2,1)}, f32[48128,128]{1,0:T(8,128)}, f32[8192,128]{1,0:T(8,128)}, f32[8192,128]{1,0:T(8,128)}, f32[3,8,128]{2,1,0:T(8,128)}) custom-call(bf16[32152,2048]{1,0:T(8,128)(2,1)} %table.1, bf16[2816,2048]{1,0:T(8,128)(2,1)} %pick_rows.1.picked, f32[1,2048]{1,0:T(1,128)S(1)} %bitcast.36, ...), custom_call_target="tpu_custom_call" | custom-call | tf_op jit(solution)/shard_map/broadcast_project/pallas_call | solution.py:479
  182.3 1.4 compare_reduce_fusion
  184.9 0.0 copy-done.6
  184.9 46.4 %conditional.1 = (bf16[1024,2048]{1,0:T(8,128)(2,1)}, bf16[8192,1,256]{2,0,1:T(8,128)(2,1)}, bf16[8192,1,256]{2,0,1:T(8,128)(2,1)}, bf16[8192,1,256]{2,0,1:T(8,128)(2,1)}) conditional(s32[]{:T(128)} %convert_element_type.55, (s32[8192]{0:T(1024)S(1)}, bf16[32152,2048]{1,0:T(8,128)(2,1)}, f32[2048]{0:T(1024)S(1)}, bf16[2048,256]{1,0:T(8,128)(2,1)}, ...), branch_computations={%region_2.5_spmd, %region_5.6_spmd} | conditional | flops 25873674240 | bytes 695641216 | solution.py:592
  185.2 27.2 %token_order.1 = (bf16[8192,256]{1,0:T(8,128)(2,1)}, bf16[8192,256]{1,0:T(8,128)(2,1)}, bf16[8192,256]{1,0:T(8,128)(2,1)}) custom-call(s32[8192]{0:T(1024)S(1)} %bitcast.32, f32[48128,128]{1,0:T(8,128)} %get-tuple-element.39.linear_in, f32[8192,128]{1,0:T(8,128)} %get-tuple-element.40.cosines, f32[8192,128]{1,0:T(8,128)} %get-tuple-element.41.sines), custom_call_target="tpu_custom_call" | custom-call | tf_op jit(solution)/shard_map/cond/branch_1_fun/token_order/pallas_call | solution.py:547
  212.4 0.7 pad_add_fusion.params
  213.0 18.3 %residual_rows.1 = bf16[1024,2048]{1,0:T(8,128)(2,1)} custom-call(s32[2]{0:T(128)} %pad_add_fusion.params, s32[8192]{0:T(1024)S(1)} %bitcast.33, s32[64,128]{1,0:T(8,128)S(1)} %get-tuple-element.37.lanes_list, bf16[6016,2048]{1,0:T(8,128)(2,1)} %get-tuple-element.38.source), custom_call_target="tpu_custom_call" | custom-call | tf_op jit(solution)/shard_map/cond/branch_1_fun/residual_rows/pallas_call | solution.py:193
Async XLA Ops:
  10.1 4.8 %copy-start.10 = (s32[8,1]{1,0:T(8,128)S(1)}, s32[8,1]{1,0:T(8,128)}, u32[]{:S(2)}) copy-start(s32[8,1]{1,0:T(8,128)} %constant.76) | copy-start | bytes 100
  10.1 4.9 %copy-start.11 = (s32[8,128]{1,0:T(8,128)S(1)}, s32[8,128]{1,0:T(8,128)}, u32[]{:S(2)}) copy-start(s32[8,128]{1,0:T(8,128)} %get-tuple-element.57) | copy-start | bytes 12292
  10.1 6.7 %copy-start = (bf16[2048,256]{1,0:T(8,128)(2,1)S(1)}, bf16[2048,256]{1,0:T(8,128)(2,1)}, u32[]{:S(2)}) copy-start(bf16[2048,256]{1,0:T(8,128)(2,1)} %w_query.1) | copy-start | bytes 3145732
  10.1 6.8 %copy-start.2 = (bf16[2048,256]{1,0:T(8,128)(2,1)S(1)}, bf16[2048,256]{1,0:T(8,128)(2,1)}, u32[]{:S(2)}) copy-start(bf16[2048,256]{1,0:T(8,128)(2,1)} %w_key.1) | copy-start | bytes 3145732
  10.1 6.7 %copy-start.4 = (bf16[2048,256]{1,0:T(8,128)(2,1)S(1)}, bf16[2048,256]{1,0:T(8,128)(2,1)}, u32[]{:S(2)}) copy-start(bf16[2048,256]{1,0:T(8,128)(2,1)} %w_value.1) | copy-start | bytes 3145732
  10.1 6.7 %copy-start.7 = (s32[8192]{0:T(1024)S(1)}, s32[8192]{0:T(1024)}, u32[]{:S(2)}) copy-start(s32[8192]{0:T(1024)} %param.11) | copy-start | bytes 98308
  10.1 6.7 %copy-start.9 = (f32[2048]{0:T(1024)S(1)}, f32[2048]{0:T(1024)}, u32[]{:S(2)}) copy-start(f32[2048]{0:T(1024)} %param.13) | copy-start | bytes 24580
  16.9 168.1 %copy-start.6 = (s32[8192]{0:T(1024)S(1)}, s32[8192]{0:T(1024)}, u32[]{:S(2)}) copy-start(s32[8192]{0:T(1024)} %param.10) | copy-start | bytes 98308

commit v3 on v2

--- a/solution.py
+++ b/solution.py
@@ -17,7 +17,7 @@
 
 CHUNK = 64
 HOT = 1024
-LIST_CAP = (2816, 640, 384, 384, 192, 192, 192, 192)
+LIST_CAP = (2816, 640, 320, 320, 192, 192, 192, 192)
 SEG_ROWS = tuple(c + (HOT if d == 0 else 0) for d, c in enumerate(LIST_CAP))
 SEG_BASE = tuple(sum(SEG_ROWS[:d]) for d in range(8))
 ROWS = sum(SEG_ROWS)
@@ -71,7 +71,7 @@
     return residual, project(w_query, HEAD_DIM ** -0.5), project(w_key, 1.0), value_heads
 
 
-def plan_kernel(vocab_rows, ids_ref, index_out, list_out, counts_out, own_place, own_high, own_low):
+def plan_kernel(vocab_rows, ids_ref, index_out, list_out, flags_out, steps_out, own_place, own_high, own_low):
     me = lax.axis_index("tp")
     ids = ids_ref[...]
     rows, lanes = ids.shape
@@ -90,14 +90,18 @@
     lower = (lax.broadcasted_iota(I32, (rows, rows), 0) > lax.broadcasted_iota(I32, (rows, rows), 1)).astype(F32).astype(BF16)
     index = jnp.where(hot, ids, 0).astype(F32)
     place = jnp.zeros((rows, lanes), F32)
+    fits = jnp.ones((1, lanes), F32)
     for d in range(8):
         here = slice(rows * d, rows * d + rows)
         before = jnp.dot(lower, per_row[here].astype(BF16), preferred_element_type=F32)
         at = within[here] + before
         place += marks[d] * at
         index += marks[d] * (at + float(SEG_BASE[d] + (HOT if d == 0 else 0)))
-        counts_out[d:d + 1, :] = jnp.sum(per_row[here], axis=0, keepdims=True).astype(I32)
+        fits *= (jnp.sum(per_row[here], axis=0, keepdims=True) <= float(LIST_CAP[d])).astype(F32)
     index_out[...] = jnp.clip(index.astype(I32), 0, ROWS - 1)
+    flags_out[...] = jnp.broadcast_to(fits, flags_out.shape)
+    length = jnp.sum((owner == me).astype(F32)).astype(I32)
+    steps_out[0] = jnp.minimum(lax.shift_right_logical(length + 127, 7), LIST_LEN // 128)
     local = ids - me * vocab_rows
     own_place[...] = jnp.where(owner == me, place.astype(I32), -1)
     own_high[...] = lax.shift_right_logical(local, 8).astype(F32)
@@ -124,8 +128,10 @@
         out_shape=(
             jax.ShapeDtypeStruct(square, I32),
             jax.ShapeDtypeStruct((LIST_LEN // 128, 128), I32),
-            jax.ShapeDtypeStruct((8, 128), I32),
+            jax.ShapeDtypeStruct((8, 128), F32),
+            jax.ShapeDtypeStruct((1,), I32),
         ),
+        out_specs=tuple(pl.BlockSpec(memory_space=space) for space in (pltpu.VMEM, pltpu.VMEM, pltpu.VMEM, pltpu.SMEM)),
         scratch_shapes=[pltpu.VMEM(square, I32), pltpu.VMEM(square, F32), pltpu.VMEM(square, F32)],
         name="plan",
     )(token_ids.reshape(square))
@@ -135,30 +141,30 @@
 DEPTH = 4
 
 
-def gather_kernel(scale, params, rows_list, lanes_list, source, out, groups, picked, in_sems, out_sems):
-    first, end = params[0], params[1]
+def gather(scale, first, end, rows_list, lanes_list, source, out, groups, picked, in_sems, out_sems):
+    def one(at, slot, t):
+        group = lax.shift_right_logical(rows_list[at + t], 3)
+        pltpu.make_async_copy(source.at[pl.ds(pl.multiple_of(group * 8, 8), 8)], groups.at[slot, pl.ds(pl.multiple_of(t * 8, 8), 8)], in_sems.at[slot]).start()
 
     def issue(step, slot):
-        def one(t, _):
-            group = lax.shift_right_logical(rows_list[(first + step) * STEP + t], 3)
-            pltpu.make_async_copy(source.at[pl.ds(pl.multiple_of(group * 8, 8), 8)], groups.at[slot, pl.ds(pl.multiple_of(t * 8, 8), 8)], in_sems.at[slot]).start()
+        def some(i, _):
+            for u in range(16):
+                one((first + step) * STEP, slot, i * 16 + u)
             return 0
 
-        lax.fori_loop(0, STEP, one, 0, unroll=8)
-
-    def arrive(slot):
-        pltpu.make_async_copy(source.at[pl.ds(0, STEP * 8)], groups.at[slot], in_sems.at[slot]).wait()
+        lax.fori_loop(0, STEP // 16, some, 0)
 
     def drain(slot):
         pltpu.make_async_copy(picked.at[slot], out.at[pl.ds(0, STEP)], out_sems.at[slot]).wait()
 
-    for ahead in range(DEPTH - 1):
-        pl.when(ahead < end)(functools.partial(issue, ahead, ahead))
+    def opening():
+        for ahead in range(DEPTH - 1):
+            pl.when(ahead < end)(functools.partial(issue, ahead, ahead))
 
     def body(step, _):
         slot, put = lax.rem(step, DEPTH), lax.rem(step, 2)
         free = lax.rem(step + DEPTH - 1, DEPTH)
-        arrive(slot)
+        pltpu.make_async_copy(source.at[pl.ds(0, STEP * 8)], groups.at[slot], in_sems.at[slot]).wait()
 
         @pl.when(step + DEPTH - 1 < end)
         def _():
@@ -173,41 +179,50 @@
         target = jnp.broadcast_to(target, (STEP, STEP)).T
         lane = lax.broadcasted_iota(I32, (STEP, STEP), 1)
         select = jnp.concatenate([(lane + STEP * j == target).astype(F32).astype(BF16) for j in range(8)], axis=1)
-        for c in range(8):
-            rows = jnp.dot(select, groups[slot, :, 256 * c:256 * c + 256], preferred_element_type=F32)
-            picked[put, :, 256 * c:256 * c + 256] = (rows if scale is None else rows * scale).astype(BF16)
+        for c in range(0, 2048, 256):
+            rows = jnp.dot(select, groups[slot, :, c:c + 256], preferred_element_type=F32)
+            picked[put, :, c:c + 256] = (rows if scale is None else rows * scale).astype(BF16)
         pltpu.make_async_copy(picked.at[put], out.at[pl.ds(pl.multiple_of(step * STEP, STEP), STEP)], out_sems.at[put]).start()
         return 0
 
+    def close():
+        @pl.when(end >= 2)
+        def _():
+            drain(lax.rem(end, 2))
+
+        @pl.when(end >= 1)
+        def _():
+            drain(lax.rem(end + 1, 2))
+
+    return opening, body, close
+
+
+GATHER_SCRATCH = [
+    pltpu.VMEM((DEPTH, STEP * 8, 2048), BF16),
+    pltpu.VMEM((2, STEP, 2048), BF16),
+    pltpu.SemaphoreType.DMA((DEPTH,)),
+    pltpu.SemaphoreType.DMA((2,)),
+]
+
+
+def pick_kernel(steps, rows_list, lanes_list, source, out, *scratch):
+    end = steps[0]
+    opening, body, close = gather(None, 0, end, rows_list, lanes_list, source, out, *scratch)
+    opening()
     lax.fori_loop(0, end, body, 0)
-    @pl.when(end >= 2)
-    def _():
-        drain(lax.rem(end, 2))
-
-    @pl.when(end >= 1)
-    def _():
-        drain(lax.rem(end + 1, 2))
-
-
-def gather_rows(params, rows_list, source, out_rows, scale, name):
+    close()
+
+
+def pick_rows(steps, rows_list, source):
+    smem, vmem, anywhere = (pl.BlockSpec(memory_space=space) for space in (pltpu.SMEM, pltpu.VMEM, pl.ANY))
     return pl.pallas_call(
-        functools.partial(gather_kernel, scale),
-        out_shape=jax.ShapeDtypeStruct((out_rows, source.shape[1]), BF16),
-        in_specs=[
-            pl.BlockSpec(memory_space=pltpu.SMEM),
-            pl.BlockSpec(memory_space=pltpu.SMEM),
-            pl.BlockSpec(memory_space=pltpu.VMEM),
-            pl.BlockSpec(memory_space=pl.ANY),
-        ],
-        out_specs=pl.BlockSpec(memory_space=pl.ANY),
-        scratch_shapes=[
-            pltpu.VMEM((DEPTH, STEP * 8, 2048), BF16),
-            pltpu.VMEM((2, STEP, 2048), BF16),
-            pltpu.SemaphoreType.DMA((DEPTH,)),
-            pltpu.SemaphoreType.DMA((2,)),
-        ],
-        name=name,
-    )(params, rows_list.reshape(-1), rows_list, source)
+        pick_kernel,
+        out_shape=jax.ShapeDtypeStruct((LIST_LEN, source.shape[1]), BF16),
+        in_specs=[smem, smem, vmem, anywhere],
+        out_specs=anywhere,
+        scratch_shapes=GATHER_SCRATCH,
+        name="pick_rows",
+    )(steps, rows_list.reshape(-1), rows_list, source)
 
 
 def ring_device(core, place):
@@ -252,7 +267,7 @@
 
 def broadcast_kernel(scale, table, picked, norm_scale, w_query, w_key, w_value, positions, flags,
                      rows_out, linear_out, cos_out, sin_out, flags_out,
-                     rows, linear, angles, ring_sems, pair_sems, recv_sems, load_sem, rows_sem, linear_sem, angle_sems, flag_sends, flag_recvs):
+                     rows, linear, angles, flags_in, ring_sems, pair_sems, recv_sems, load_sem, rows_sem, linear_sem, angle_sems, flag_sends, flag_recvs):
     me, plane = lax.axis_index("tp"), lax.axis_index("dp")
     core, chip = me % 2, me // 2
     x, y = chip % 2, chip // 2
@@ -281,17 +296,27 @@
     @pl.when(me == 0)
     def _():
         def load_hot(number, _):
+            load_list(SPLIT + number, 0)
             pltpu.make_async_copy(table.at[chunk(number)], rows.at[chunk(number)], load_sem.at[number]).start()
             return 0
 
+        def load_both(number, _):
+            load_list(SPLIT + number, 0)
+            return load_list(number, 0)
+
         lax.fori_loop(0, HOT // CHUNK, load_hot, 0)
-
-    lax.fori_loop(own_list, own_end, load_list, 0)
+        lax.fori_loop(HOT // CHUNK, SEG_CHUNKS[0] - SPLIT, load_both, 0)
+        lax.fori_loop(SEG_CHUNKS[0] - SPLIT, SPLIT, load_list, 0)
+
+    @pl.when(me != 0)
+    def _():
+        lax.fori_loop(own_list, own_end, load_list, 0)
+
     pl.semaphore_wait(barrier, 6)
 
     def flag_copy(hop):
         return pltpu.make_async_remote_copy(
-            src_ref=flags, dst_ref=flags_out.at[hop], send_sem=flag_sends.at[hop], recv_sem=flag_recvs.at[hop],
+            src_ref=flags, dst_ref=flags_in.at[hop], send_sem=flag_sends.at[hop], recv_sem=flag_recvs.at[hop],
             device_id={"dp": (plane + hop + 1) % 4}, device_id_type=MESH)
 
     for hop in range(3):
@@ -440,6 +465,7 @@
     put_linear(STEPS - 1)
     for hop in range(3):
         flag_copy(hop).wait()
+    flags_out[...] = jnp.minimum(jnp.minimum(flags[...], flags_in[0]), jnp.minimum(flags_in[1], flags_in[2]))
 
     def sent_to_ring(step, _):
         copy(number_at(step, RING_RUNS), ring_sems, after).wait_send()
@@ -483,7 +509,7 @@
             jax.ShapeDtypeStruct((ROWS * 8, 128), F32),
             jax.ShapeDtypeStruct((tokens, 128), F32),
             jax.ShapeDtypeStruct((tokens, 128), F32),
-            jax.ShapeDtypeStruct((3, 8, 128), F32),
+            jax.ShapeDtypeStruct((8, 128), F32),
         ),
         in_specs=[anywhere, anywhere] + [vmem] * 6,
         out_specs=(anywhere, anywhere, anywhere, anywhere, vmem),
@@ -491,6 +517,7 @@
             pltpu.VMEM((ROWS, 2048), BF16),
             pltpu.VMEM((ROWS * 8, 128), F32),
             pltpu.VMEM((2, 2, 128, 128), F32),
+            pltpu.VMEM((3, 8, 128), F32),
             pltpu.SemaphoreType.DMA((ALL_CHUNKS,)),
             pltpu.SemaphoreType.DMA((ALL_CHUNKS,)),
             pltpu.SemaphoreType.DMA((ALL_CHUNKS,)),
@@ -506,19 +533,29 @@
     )(table, picked, norm_scale.reshape(1, -1), w_query, w_key, w_value, positions, flags)
 
 
-TOKEN_BLOCK = 512
+TOKEN_BLOCK = 1024
 OUT_PITCH = TOKEN_BLOCK + 4
 
 
-def order_kernel(index, linear_in, cosines, sines, q_out, k_out, v_out, linear, turned, sems):
+def order_kernel(scale, index, index_lanes, rows, linear_in, cosines, sines, resid_out, q_out, k_out, v_out, linear, turned, sems, *scratch):
     step = pl.program_id(0)
+    own_steps = jnp.asarray(resid_out.shape[0] // STEP, I32)
+    opening, body, close = gather(scale, lax.axis_index("tp") * own_steps, own_steps, index, index_lanes, rows, resid_out, *scratch)
+
+    copies = [pltpu.make_async_copy(linear_in.at[pl.ds(j * ROWS, ROWS)], linear.at[pl.ds(j * ROWS, ROWS)], sems.at[j]) for j in range(8)]
 
     @pl.when(step == 0)
     def _():
-        eighth = ROWS
-        copies = [pltpu.make_async_copy(linear_in.at[pl.ds(j * eighth, eighth)], linear.at[pl.ds(j * eighth, eighth)], sems.at[j]) for j in range(8)]
+        opening()
         for c in copies:
             c.start()
+
+    @pl.when(step < own_steps)
+    def _():
+        body(step, 0)
+
+    @pl.when(step == 0)
+    def _():
         for c in copies:
             c.wait()
 
@@ -538,59 +575,50 @@
     k_out[:, 128:] = (part[3] * cos + part[2] * sin).astype(BF16)
     v_out[:, :128] = part[4].astype(BF16)
     v_out[:, 128:] = part[5].astype(BF16)
-
-
-def token_order(index, linear, cosines, sines):
+    pl.when(step == pl.num_programs(0) - 1)(close)
+
+
+def token_order(index, rows, linear, cosines, sines, scale):
     tokens = cosines.shape[0]
     by_token = lambda i, idx: (i, 0)
     out = jax.ShapeDtypeStruct((tokens, HEAD_DIM), BF16)
+    vmem, anywhere = (pl.BlockSpec(memory_space=space) for space in (pltpu.VMEM, pl.ANY))
     return pl.pallas_call(
-        order_kernel,
-        out_shape=(out, out, out),
+        functools.partial(order_kernel, scale),
+        out_shape=(jax.ShapeDtypeStruct((tokens // 8, rows.shape[1]), BF16), out, out, out),
         grid_spec=pltpu.PrefetchScalarGridSpec(
             num_scalar_prefetch=1,
             grid=(tokens // TOKEN_BLOCK,),
             in_specs=[
-                pl.BlockSpec(memory_space=pl.ANY),
+                vmem, anywhere, anywhere,
                 pl.BlockSpec((TOKEN_BLOCK, 128), by_token),
                 pl.BlockSpec((TOKEN_BLOCK, 128), by_token),
             ],
-            out_specs=[pl.BlockSpec((TOKEN_BLOCK, HEAD_DIM), by_token)] * 3,
-            scratch_shapes=[pltpu.VMEM((8 * ROWS, 128), F32), pltpu.VMEM((8 * OUT_PITCH, 128), F32), pltpu.SemaphoreType.DMA((8,))],
+            out_specs=[anywhere] + [pl.BlockSpec((TOKEN_BLOCK, HEAD_DIM), by_token)] * 3,
+            scratch_shapes=[pltpu.VMEM((8 * ROWS, 128), F32), pltpu.VMEM((8 * OUT_PITCH, 128), F32), pltpu.SemaphoreType.DMA((8,))] + GATHER_SCRATCH,
         ),
-        compiler_params=pltpu.CompilerParams(dimension_semantics=("arbitrary",), vmem_limit_bytes=48 * 2 ** 20),
+        compiler_params=pltpu.CompilerParams(dimension_semantics=("arbitrary",), vmem_limit_bytes=60 * 2 ** 20),
         name="token_order",
-    )(index, linear, cosines, sines)
+    )(index.reshape(tokens), index, rows, linear, cosines, sines)
 
 
 def solution(mesh):
     def local_step(token_ids, positions, table_rows, norm_scale, w_query, w_key, w_value):
-        me = lax.axis_index("tp")
         vocab_rows, model_width = table_rows.shape
         scale = float(np.asarray(math.sqrt(model_width)).astype(BF16))
-        tokens = token_ids.shape[0]
-        index, own_list, counts = plan(token_ids, vocab_rows)
-        length = counts[:, 0]
-        fits = jnp.all(length <= jnp.asarray(LIST_CAP, I32))
-        steps = jnp.minimum((length[me] + STEP - 1) // STEP, LIST_LEN // STEP)
-        picked = gather_rows(jnp.stack([0, steps]).astype(I32), own_list, table_rows, LIST_LEN, None, "pick_rows")
-        flags = jnp.broadcast_to(fits.astype(F32), (8, 128))
-        rows, linear, cosines, sines, others = broadcast_project(
+        index, own_list, flags, steps = plan(token_ids, vocab_rows)
+        picked = pick_rows(steps, own_list, table_rows)
+        rows, linear, cosines, sines, flags = broadcast_project(
             table_rows, picked, norm_scale, w_query, w_key, w_value, positions.reshape(-1, 128), flags, scale)
-        fits_all = fits & jnp.all(others[:, 0, 0] > 0.5)
 
         def compact_step(token_ids, positions, table_rows, norm_scale, w_query, w_key, w_value, index, rows, linear, cosines, sines):
-            own_tokens = tokens // 8
-            resid_params = jnp.stack([me * (own_tokens // STEP), own_tokens // STEP]).astype(I32)
-            residual = gather_rows(resid_params, index, rows, own_tokens, scale, "residual_rows")
-            queries, keys, values = token_order(index.reshape(tokens), linear, cosines, sines)
-            return residual, queries, keys, values
+            return token_order(index, rows, linear, cosines, sines, scale)
 
         def dense(token_ids, positions, table_rows, norm_scale, w_query, w_key, w_value, *_):
             return dense_step(token_ids, positions, table_rows, norm_scale, w_query, w_key, w_value)
 
         residual, queries, keys, values = lax.cond(
-            fits_all, compact_step, dense,
+            flags[0, 0] > 0.5, compact_step, dense,
             token_ids, positions, table_rows, norm_scale, w_query, w_key, w_value, index, rows, linear, cosines, sines)
         return residual, queries[:, None, :], keys[:, None, :], values[:, None, :]
 

time: 236 us -> 216 us (0.915); the launches traced: 232 us -> 216 us
  Pallas kernels: 221 us -> 213 us
  other arithmetic: 4.42 us -> 0 us
  between operations: 5.46 us -> 1.58 us
    pallas_call x3 -> x2, Pallas kernels: 50.3 us -> 43 us  [the longest x1 37.1 us: token_order(): pl.pallas_call(functools.partial(order_kernel, scale), out_shape=(jax.Sha...]
where the time goes in v3:
time: 216 us
  Pallas kernels  213 us (99%)
    pallas_call x1, Pallas kernels, broadcast_project(): pl.pallas_call(functools.partial(broadcast_kernel, scale), out_shape=(jax...  164 us
    pallas_call x1, Pallas kernels, token_order(): pl.pallas_call(functools.partial(order_kernel, scale), out_shape=(jax.Sha...  37.1 us
    pallas_call x1, Pallas kernels, pick_rows(): pl.pallas_call(pick_kernel, out_shape=jax.ShapeDtypeStruct((LIST_LEN, sou...  5.9 us
    pallas_call x1, Pallas kernels, plan(): pl.pallas_call(functools.partial(plan_kernel, vocab_rows), out_shape=(jax...  5.06 us

profile of v3, /device:TPU:15, one launch (start us, length us, event | category | flops | bytes accessed | tf_op | source)
XLA Modules:
  0.0 215.5 jit_solution(1593020399525871851)
XLA Ops:
  0.6 5.1 %plan.1 = (s32[64,128]{1,0:T(8,128)S(1)}, s32[22,128]{1,0:T(8,128)}, f32[8,128]{1,0:T(8,128)}, s32[1]{0:T(128)}) custom-call(s32[64,128]{1,0:T(8,128)} %bitcast.28), custom_call_target="tpu_custom_call" | custom-call | tf_op jit(solution)/shard_map/plan/pallas_call | solution.py:126
  5.7 0.0 copy-start
  5.7 0.0 copy-start.2
  5.7 0.0 copy-start.4
  5.7 0.0 copy-start.7
  5.7 0.0 copy-start.9
  5.8 5.9 %pick_rows.1.picked = bf16[2816,2048]{1,0:T(8,128)(2,1)} custom-call(s32[1]{0:T(128)} %get-tuple-element.60.steps, s32[2816]{0:T(1024)} %bitcast.31, s32[22,128]{1,0:T(8,128)} %get-tuple-element.61.lanes_list, bf16[32152,2048]{1,0:T(8,128)(2,1)} %table.1), custom_call_target="tpu_custom_call" | custom-call | tf_op jit(solution)/shard_map/pick_rows/pallas_call | solution.py:218
  11.7 0.0 copy-done
  11.7 0.0 copy-done.2
  11.7 0.0 copy-done.4
  11.7 0.0 copy-done.7
  11.7 0.0 copy-done.9
  11.7 0.0 copy-start.6
  11.7 164.5 %broadcast_project.1 = (bf16[5888,2048]{1,0:T(8,128)(2,1)}, f32[47104,128]{1,0:T(8,128)}, f32[8192,128]{1,0:T(8,128)}, f32[8192,128]{1,0:T(8,128)}, f32[8,128]{1,0:T(8,128)}) custom-call(bf16[32152,2048]{1,0:T(8,128)(2,1)} %table.1, bf16[2816,2048]{1,0:T(8,128)(2,1)} %pick_rows.1.picked, f32[1,2048]{1,0:T(1,128)S(1)} %bitcast.32, ...), custom_call_target="tpu_custom_call" | custom-call | tf_op jit(solution)/shard_map/broadcast_project/pallas_call | solution.py:505
  176.2 1.2 slice.15
  178.0 0.0 copy-done.6
  178.0 37.3 %conditional.1 = (bf16[1024,2048]{1,0:T(8,128)(2,1)}, bf16[8192,1,256]{2,0,1:T(8,128)(2,1)}, bf16[8192,1,256]{2,0,1:T(8,128)(2,1)}, bf16[8192,1,256]{2,0,1:T(8,128)(2,1)}) conditional(s32[]{:T(128)} %bitcast.15, (s32[8192]{0:T(1024)S(1)}, bf16[32152,2048]{1,0:T(8,128)(2,1)}, f32[2048]{0:T(1024)S(1)}, bf16[2048,256]{1,0:T(8,128)(2,1)}, ...), branch_computations={%region_0.3_spmd, %region_3.4_spmd} | conditional | flops 25873674240 | bytes 695641216 | solution.py:620
  178.3 37.1 %token_order.1 = (bf16[1024,2048]{1,0:T(8,128)(2,1)}, bf16[8192,256]{1,0:T(8,128)(2,1)}, bf16[8192,256]{1,0:T(8,128)(2,1)}, bf16[8192,256]{1,0:T(8,128)(2,1)}) custom-call(s32[8192]{0:T(1024)S(1)} %bitcast.29, s32[64,128]{1,0:T(8,128)S(1)} %get-tuple-element.38.index_lanes, bf16[5888,2048]{1,0:T(8,128)(2,1)} %get-tuple-element.39.rows, ...), custom_call_target="tpu_custom_call" | custom-call | tf_op jit(solution)/shard_map/cond/branch_1_fun/token_order/pallas_call | solution.py:586
Async XLA Ops:
  5.7 6.0 %copy-start = (bf16[2048,256]{1,0:T(8,128)(2,1)S(1)}, bf16[2048,256]{1,0:T(8,128)(2,1)}, u32[]{:S(2)}) copy-start(bf16[2048,256]{1,0:T(8,128)(2,1)} %w_query.1) | copy-start | bytes 3145732
  5.7 6.0 %copy-start.2 = (bf16[2048,256]{1,0:T(8,128)(2,1)S(1)}, bf16[2048,256]{1,0:T(8,128)(2,1)}, u32[]{:S(2)}) copy-start(bf16[2048,256]{1,0:T(8,128)(2,1)} %w_key.1) | copy-start | bytes 3145732
  5.7 6.0 %copy-start.4 = (bf16[2048,256]{1,0:T(8,128)(2,1)S(1)}, bf16[2048,256]{1,0:T(8,128)(2,1)}, u32[]{:S(2)}) copy-start(bf16[2048,256]{1,0:T(8,128)(2,1)} %w_value.1) | copy-start | bytes 3145732
  5.7 6.0 %copy-start.7 = (s32[8192]{0:T(1024)S(1)}, s32[8192]{0:T(1024)}, u32[]{:S(2)}) copy-start(s32[8192]{0:T(1024)} %param.10) | copy-start | bytes 98308
  5.7 6.0 %copy-start.9 = (f32[2048]{0:T(1024)S(1)}, f32[2048]{0:T(1024)}, u32[]{:S(2)}) copy-start(f32[2048]{0:T(1024)} %param.12) | copy-start | bytes 24580
  11.7 166.3 %copy-start.6 = (s32[8192]{0:T(1024)S(1)}, s32[8192]{0:T(1024)}, u32[]{:S(2)}) copy-start(s32[8192]{0:T(1024)} %param.9) | copy-start | bytes 98308
